TPU v7x, 8 devices: a whole 2x2x1 slice. The times are simulated.
8 devices in a mesh: dp: 1 (over z), sp: 8 (over y, x, core).
Axes of the slice: x: 2, y: 2, z: 1, core: 2. Of those that a mesh axis runs over, the one named last changes fastest.
Arguments:
- x_in: bfloat16 [4, 2048, 2048], P('dp', 'sp')
- positions: int32 [4, 2048], P('dp', 'sp')
- keep_mask: int32 [4, 2048], P('dp', 'sp')
- ln_gain: float32 [2048], replicated
- ln_bias: float32 [2048], replicated
- w_qkv: bfloat16 [2048, 16, 3, 128], replicated
- b_qkv: float32 [16, 3, 128], replicated
- w_out: bfloat16 [2048, 2048], replicated
- b_out: float32 [2048], replicated
- grad_y: bfloat16 [4, 2048, 2048], P('dp', 'sp')
Outputs:
- output 1: bfloat16 [4, 2048, 2048], P('dp', 'sp')
- output 2: bfloat16 [4, 2048, 2048], P('dp', 'sp')
- output 3: float32 [2048, 16, 3, 128], P('dp')
- output 4: float32 [16, 3, 128], P('dp')
- output 5: float32 [2048, 2048], P('dp')
- output 6: float32 [2048], P('dp')
- output 7: float32 [2048], P('dp')
- output 8: float32 [2048], P('dp')
All inputs are finite; a program needn't handle non-finite values.
Results may differ from a plain program's by a relative error of at most 0.00988608.
Values are sent between devices in bfloat16 or wider.
A program may use at most 1 GiB of HBM per device.

v0:
```python
import jax
import jax.numpy as jnp
from jax import lax
from jax.sharding import PartitionSpec as P

NORM_EPS = 1e-5
MASK_FILL = -1e30


def norm_forward(x_blk, ln_gain, ln_bias):
    x_f32 = x_blk.astype(jnp.float32)
    centered = x_f32 - jnp.mean(x_f32, axis=-1, keepdims=True)
    inv_std = lax.rsqrt(jnp.mean(centered * centered, axis=-1, keepdims=True) + NORM_EPS)
    x_hat = centered * inv_std
    x_norm = (x_hat * ln_gain + ln_bias).astype(jnp.bfloat16)
    return x_f32, x_hat, inv_std, x_norm


def norm_backward(d_norm, x_hat, inv_std, ln_gain):
    d_hat = d_norm * ln_gain
    d_mean = jnp.mean(d_hat, axis=-1, keepdims=True)
    d_proj = jnp.mean(d_hat * x_hat, axis=-1, keepdims=True)
    return inv_std * (d_hat - d_mean - x_hat * d_proj)


def attn_probs(q_part, k_part, q_pos, k_pos, k_keep, q_index, k_index, slopes, qk_scale):
    scores = jnp.einsum("bqnd,bknd->bnqk", q_part, k_part, preferred_element_type=jnp.float32) * qk_scale
    pos_gap = (q_pos[:, :, None] - k_pos[:, None, :]).astype(jnp.float32)
    scores = scores - slopes[None, :, None, None] * pos_gap[:, None, :, :]
    allowed = (k_index[None, :] <= q_index[:, None])[None, None] & (k_keep[:, None, None, :] > 0)
    return jax.nn.softmax(jnp.where(allowed, scores, MASK_FILL), axis=-1)


def attn_backward(attn_prob, prob_lo, q_part, k_part, v_part, o_part, do_part, qk_scale):
    dv_part = jnp.einsum("bnqk,bqnd->bknd", prob_lo, do_part, preferred_element_type=jnp.float32)
    grad_prob = jnp.einsum("bqnd,bknd->bnqk", do_part, v_part, preferred_element_type=jnp.float32)
    row_dot = jnp.einsum("bqnd,bqnd->bnq", do_part, o_part, preferred_element_type=jnp.float32)
    ds_lo = (attn_prob * (grad_prob - row_dot[:, :, :, None])).astype(jnp.bfloat16)
    dq_part = jnp.einsum("bnqk,bknd->bqnd", ds_lo, k_part, preferred_element_type=jnp.float32) * qk_scale
    dk_part = jnp.einsum("bnqk,bqnd->bknd", ds_lo, q_part, preferred_element_type=jnp.float32) * qk_scale
    return dq_part, dk_part, dv_part


def solution(mesh):
    sp_size = mesh.shape["sp"]

    def block_fn(x_blk, pos_blk, keep_blk, ln_gain, ln_bias, w_qkv, b_qkv, w_out, b_out, dy_blk):
        batch_loc, seq_loc, hidden = x_blk.shape
        num_heads = w_qkv.shape[1]
        head_dim = w_qkv.shape[3]
        heads_loc = num_heads // sp_size
        seq_len = seq_loc * sp_size
        qk_scale = head_dim ** -0.5
        sp_rank = lax.axis_index("sp")
        x_f32, x_hat, inv_std, x_norm = norm_forward(x_blk, ln_gain, ln_bias)
        qkv_loc = (jnp.einsum("bsh,hnct->bsnct", x_norm, w_qkv, preferred_element_type=jnp.float32) + b_qkv).astype(jnp.bfloat16)
        qkv_head = lax.all_to_all(qkv_loc, "sp", 2, 1, tiled=True)
        pos_full = lax.all_gather(pos_blk, "sp", axis=1, tiled=True)
        keep_full = lax.all_gather(keep_blk, "sp", axis=1, tiled=True)
        q_head = qkv_head[:, :, :, 0]
        k_head = qkv_head[:, :, :, 1]
        v_head = qkv_head[:, :, :, 2]
        head_ids = sp_rank * heads_loc + jnp.arange(heads_loc)
        slopes = jnp.exp2(-8.0 * (head_ids + 1).astype(jnp.float32) / num_heads)
        tok_index = jnp.arange(seq_len)
        attn_prob = attn_probs(q_head, k_head, pos_full, pos_full, keep_full, tok_index, tok_index, slopes, qk_scale)
        prob_lo = attn_prob.astype(jnp.bfloat16)
        o_head = jnp.einsum("bnqk,bknd->bqnd", prob_lo, v_head, preferred_element_type=jnp.float32).astype(jnp.bfloat16)
        o_loc = lax.all_to_all(o_head, "sp", 1, 2, tiled=True).reshape(batch_loc, seq_loc, hidden)
        y_blk = (x_f32 + jnp.einsum("bsh,hk->bsk", o_loc, w_out, preferred_element_type=jnp.float32) + b_out).astype(jnp.bfloat16)
        grad_b_out = jnp.sum(dy_blk.astype(jnp.float32), axis=(0, 1))
        grad_w_out = jnp.einsum("bsh,bsk->hk", o_loc, dy_blk, preferred_element_type=jnp.float32)
        do_loc = jnp.einsum("bsk,hk->bsh", dy_blk, w_out, preferred_element_type=jnp.float32).astype(jnp.bfloat16)
        do_head = lax.all_to_all(do_loc.reshape(batch_loc, seq_loc, num_heads, head_dim), "sp", 2, 1, tiled=True)
        dq_head, dk_head, dv_head = attn_backward(attn_prob, prob_lo, q_head, k_head, v_head, o_head, do_head, qk_scale)
        dqkv_head = jnp.stack([dq_head, dk_head, dv_head], axis=3).astype(jnp.bfloat16)
        dqkv_loc = lax.all_to_all(dqkv_head, "sp", 1, 2, tiled=True)
        grad_b_qkv = jnp.sum(dqkv_loc.astype(jnp.float32), axis=(0, 1))
        grad_w_qkv = jnp.einsum("bsh,bsnct->hnct", x_norm, dqkv_loc, preferred_element_type=jnp.float32)
        d_norm = jnp.einsum("bsnct,hnct->bsh", dqkv_loc, w_qkv, preferred_element_type=jnp.float32)
        grad_gain = jnp.sum(d_norm * x_hat, axis=(0, 1))
        grad_bias = jnp.sum(d_norm, axis=(0, 1))
        grad_x = (dy_blk.astype(jnp.float32) + norm_backward(d_norm, x_hat, inv_std, ln_gain)).astype(jnp.bfloat16)
        summed = lax.psum((grad_w_qkv, grad_b_qkv, grad_w_out, grad_b_out, grad_gain, grad_bias), "sp")
        return (y_blk, grad_x) + tuple(summed)

    act_spec = P("dp", "sp", None)
    tok_spec = P("dp", "sp")
    in_specs = (act_spec, tok_spec, tok_spec, P(), P(), P(), P(), P(), P(), act_spec)
    out_specs = (act_spec, act_spec, P("dp", None, None, None), P("dp", None, None), P("dp", None), P("dp"), P("dp"), P("dp"))
    return jax.shard_map(block_fn, mesh=mesh, in_specs=in_specs, out_specs=out_specs, check_vma=False)
```

profile of v0, /device:TPU:0, one launch (start us, length us, event | category | flops | bytes accessed | tf_op | source)
XLA Modules:
  0.0 1662.6 jit_solution(14901429541165155734)
XLA Ops:
  7.2 12.6 convert_bitcast_fusion.1
  34.0 32.4 %add_convert_fusion = bf16[4,256,16,3,128]{4,1,3,2,0:T(8,128)(2,1)} fusion(f32[16,3,128]{2,1,0:T(4,128)S(1)} %copy.64, bf16[2048,16,3,128]{3,1,2,0:T(8,128)(2,1)} %param.15, bf16[4,256,2048]{2,1,0:T(8,128)(2,1)S(1)} %copy-done.1, f32[2048]{0:T(1024)S(1)} %copy-done.13, f32[2048]{0:T(1024)S(1)} %copy-done.9, f32[4,256]{1,0:T(4,128)S(1)} %add_rsqrt_fusion, ...), kind=kOutput, calls=%fused_computation.20 | convolution fusion | flops 25794969600 | bytes 41992192 | tf_op jit(solution)/shard_map/bsh,hnct->bsnct/dot_general | solution.py:56
  78.1 12.8 all_gather.7
  108.3 21.2 %subtract_convert_fusion = f32[4,2048,2048]{1,2,0:T(8,128)} fusion(s32[4,2048]{1,0:T(4,128)S(1)} %all_gather.7), kind=kLoop, calls=%fused_computation.8 | loop fusion | flops 33554432 | bytes 67141632 | tf_op jit(solution)/shard_map/convert_element_type | solution.py:28
  156.7 88.5 %all-to-all-done = bf16[4,256,16,3,128]{4,1,3,0,2:T(8,128)(2,1)} async-done(((bf16[4,256,16,3,128]{4,1,3,0,2:T(8,128)(2,1)}), bf16[4,256,16,3,128]{4,1,3,0,2:T(8,128)(2,1)}, u32[]{:S(2)}, u32[]{:S(2)}) %all-to-all-start) | async-done | bytes 12582944 | tf_op jit(solution)/shard_map/all_to_all | solution.py:57
  255.9 95.8 %fusion.51 = (f32[4,2,2048]{2,1,0:T(2,128)S(1)}, f32[4,2,2048,2048]{2,3,1,0:T(8,128)}) fusion(f32[4,2048,2048]{1,2,0:T(8,128)} %subtract_convert_fusion, f32[2]{0:T(128)S(1)} %multiply_exponential_fusion, pred[4,2048,2048]{1,2,0:T(8,128)(4,1)} %broadcast_and_fusion, bf16[4,2048,2,3,128]{4,1,2,0,3:T(8,128)(2,1)} %bitcast.132), kind=kOutput, calls=%fused_computation.79 | convolution fusion | flops 8791263232 | bytes 226557952 | tf_op jit(solution)/shard_map/sub | solution.py:31
  351.7 64.2 %fusion.7 = bf16[4,2,2048,2048]{2,3,1,0:T(8,128)(2,1)} fusion(f32[4,2,2048,2048]{2,3,1,0:T(8,128)} %get-tuple-element.45, f32[4,2,2048]{2,1,0:T(2,128)S(1)} %get-tuple-element.44), kind=kLoop, calls=%fused_computation.12 | loop fusion | flops 67108864 | bytes 201392128 | tf_op jit(solution)/shard_map/convert_element_type | solution.py:67
  415.9 28.8 %multiply_reduce_fusion = (f32[4,2,2048]{2,1,0:T(2,128)S(1)}, bf16[4,2,128,2048]{3,2,1,0:T(8,128)(2,1)}) fusion(f32[4,2,2048,128]{2,3,1,0:T(8,128)} %copy.98, bf16[4,2,2048,2048]{2,3,1,0:T(8,128)(2,1)} %fusion.7, bf16[4,2048,2,3,128]{4,1,2,0,3:T(8,128)(2,1)} %bitcast.133), kind=kOutput, calls=%fused_computation.53 | convolution fusion | flops 8598306816 | bytes 83951616 | tf_op jit(solution)/shard_map/bnqk,bknd->bqnd/dot_general | solution.py:68
  444.7 66.9 %multiply_convert_fusion = bf16[4,2,2048,2048]{2,3,1,0:T(8,128)(2,1)} fusion(f32[4,2,2048]{2,1,0:T(2,128)S(1)} %get-tuple-element.46, f32[4,2,2048,2048]{2,3,1,0:T(8,128)} %get-tuple-element.45, f32[4,2,2048]{2,1,0:T(2,128)S(1)} %get-tuple-element.44, bf16[4,2048,2,128]{3,1,2,0:T(8,128)(2,1)} %bitcast.129, bf16[4,2048,2,3,128]{4,1,2,0,3:T(8,128)(2,1)} %bitcast.134), kind=kOutput, calls=%fused_computation.1 | convolution fusion | flops 8724152320 | bytes 209846272 | tf_op jit(solution)/shard_map/bqnd,bknd->bnqk/dot_general | solution.py:36
  511.6 33.3 %fusion.45 = bf16[4,2048,2,1,128]{1,4,2,0,3:T(8,128)(2,1)} fusion(bf16[4,2,2048,2048]{2,3,1,0:T(8,128)(2,1)} %multiply_convert_fusion, bf16[4,2048,2,3,128]{4,1,2,0,3:T(8,128)(2,1)} %bitcast.135), kind=kOutput, calls=%fused_computation.69 | convolution fusion | flops 8594128896 | bytes 75497472 | tf_op jit(solution)/shard_map/bnqk,bqnd->bknd/dot_general | solution.py:40
  544.9 26.4 %fusion.44 = bf16[4,2048,2,1,128]{1,4,2,0,3:T(8,128)(2,1)} fusion(bf16[4,2,2048,2048]{2,3,1,0:T(8,128)(2,1)} %multiply_convert_fusion, bf16[4,2048,2,3,128]{4,1,2,0,3:T(8,128)(2,1)} %bitcast.136), kind=kOutput, calls=%fused_computation.68 | convolution fusion | flops 8594128896 | bytes 75497472 | tf_op jit(solution)/shard_map/bnqk,bknd->bqnd/dot_general | solution.py:39
  585.8 33.2 %convert_bitcast_fusion = bf16[4,2048,2,1,128]{1,4,2,0,3:T(8,128)(2,1)} fusion(bf16[4,2048,2,128]{3,1,2,0:T(8,128)(2,1)} %bitcast.130, bf16[4,2,2048,2048]{2,3,1,0:T(8,128)(2,1)} %fusion.7), kind=kOutput, calls=%fused_computation.65 | convolution fusion | flops 8592031744 | bytes 75497472 | tf_op jit(solution)/shard_map/bnqk,bqnd->bknd/dot_general | solution.py:35
  628.6 31.0 %copy.80 = bf16[4,2048,2,3,128]{4,2,0,3,1:T(2,128)(2,1)} copy(bf16[4,2048,2,3,128]{1,4,2,0,3:T(8,128)(2,1)} %pad_maximum_fusion) | data formatting | bytes 25165824 | tf_op jit(solution)/shard_map/stack | solution.py:76
  678.8 15.4 convolution_bitcast_fusion.1
  694.3 108.4 %all-to-all-done.3 = bf16[4,2048,2,3,128]{4,2,0,3,1:T(2,128)(2,1)} async-done(((bf16[4,2048,2,3,128]{4,2,0,3,1:T(2,128)(2,1)}), bf16[4,2048,2,3,128]{4,2,0,3,1:T(2,128)(2,1)}, u32[]{:S(2)}, u32[]{:S(2)}) %all-to-all-start.3) | async-done | bytes 12582944 | tf_op jit(solution)/shard_map/all_to_all | solution.py:77
  802.7 11.9 copy.114
  814.6 35.6 %convolution_bitcast_fusion = f32[2048,16,3,128]{3,0,2,1:T(8,128)} fusion(bf16[4,256,16,3,128]{4,1,0,3,2:T(8,128)(2,1)} %bitcast.140, bf16[4,256,2048]{2,1,0:T(8,128)(2,1)S(1)} %copy-done.2, f32[2048]{0:T(1024)S(1)} %copy-done.14, f32[2048]{0:T(1024)S(1)} %copy-done.10, f32[4,256]{1,0:T(4,128)S(1)} %copy-done.8, f32[4,256]{1,0:T(4,128)S(1)} %copy-done.5), kind=kOutput, calls=%fused_computation.21 | convolution fusion | flops 25782386688 | bytes 67133440 | tf_op jit(solution)/shard_map/bsh,bsnct->hnct/dot_general | solution.py:79
  850.9 14.4 fusion.32
  876.8 21.7 %copy.81 = bf16[4,8,256,2,3,128]{2,1,5,3,0,4:T(8,128)(2,1)} copy(bf16[4,8,256,2,3,128]{5,3,0,4,2,1:T(2,128)(2,1)} %bitcast.28) | data formatting | bytes 25165824 | tf_op jit(solution)/shard_map/all_to_all | solution.py:77
  904.9 36.7 %fusion.28 = (f32[2048]{0:T(1024)S(1)}, f32[4,256]{1,0:T(4,128)S(1)}, f32[4,256]{1,0:T(4,128)S(1)}, f32[2048]{0:T(1024)S(1)}, f32[4,256,2048,1,1]{2,1,4,0,3:T(8,128)}) fusion(bf16[4,256,2048]{2,1,0:T(8,128)(2,1)} %param.10, f32[4,256]{1,0:T(4,128)S(1)} %copy-done.8, f32[4,256]{1,0:T(4,128)S(1)} %copy-done.5, f32[2048]{0:T(1024)S(1)} %copy-done.10, ...), kind=kOutput, calls=%fused_computation.42 | convolution fusion | flops 25790769152 | bytes 50372608 | tf_op jit(solution)/shard_map/bsnct,hnct->bsh/dot_general | solution.py:80
  950.2 24.3 %all-reduce = (f32[16,3,128]{2,0,1:T(8,128)}, f32[2048]{0:T(1024)}, f32[2048]{0:T(1024)}, f32[2048]{0:T(1024)}) all-reduce(f32[16,3,128]{2,0,1:T(8,128)S(1)} %bitcast.141, f32[2048]{0:T(1024)S(1)} %get-tuple-element.42, f32[2048]{0:T(1024)S(1)} %get-tuple-element.32, ...), channel_id=1, replica_groups=mesh['dp'=1,'sp'=8] {'sp'}, use_global_device_ids=true, to_apply=%region_8.9 | all-reduce | flops 12288 | bytes 98304 | tf_op jit(solution)/shard_map/psum | solution.py:84
  974.5 623.1 %all-reduce.4.cloned.1.call-done = (f32[2048,16,3,128]{3,0,2,1:T(8,128)}, f32[2048,2048]{1,0:T(8,128)}) async-done(((f32[2048,16,3,128]{3,0,2,1:T(8,128)}, f32[2048,2048]{1,0:T(8,128)}), (f32[2048,16,3,128]{3,0,2,1:T(8,128)}, f32[2048,2048]{1,0:T(8,128)})) %all-reduce.4.cloned.1.call-update) | async-done | bytes 67108880 | tf_op jit(solution)/shard_map/psum | solution.py:84
  1597.6 45.9 %copy.88 = f32[2048,16,3,128]{3,1,2,0:T(8,128)} copy(f32[2048,16,3,128]{3,0,2,1:T(8,128)} %get-tuple-element.40) | data formatting | bytes 100663296
  1643.5 11.8 copy.132
  (65 shorter events, 151.5 us)
Async XLA Ops:
  23.0 11.0 copy-start.6
  23.0 11.0 copy-start.9
  23.0 11.0 copy-start.13
  23.0 78.9 %all-to-all-start.2 = ((bf16[4,256,16,128]{3,1,0,2:T(8,128)(2,1)}), bf16[4,256,16,128]{3,1,0,2:T(8,128)(2,1)}, u32[]{:S(2)}, u32[]{:S(2)}) async-start(bf16[4,256,16,128]{3,1,0,2:T(8,128)(2,1)} %bitcast.137), calls=%async_computation.2 | async-start | bytes 8388608 | tf_op jit(solution)/shard_map/all_to_all | solution.py:74
  27.5 6.5 copy-start.1
  30.5 36.0 %copy-start.4 = (f32[4,256]{1,0:T(4,128)}, f32[4,256]{1,0:T(4,128)S(1)}, u32[]{:S(2)}) copy-start(f32[4,256]{1,0:T(4,128)S(1)} %broadcast_multiply_fusion.2) | copy-start | bytes 12292
  33.9 32.5 %copy-start.7 = (f32[4,256]{1,0:T(4,128)}, f32[4,256]{1,0:T(4,128)S(1)}, u32[]{:S(2)}) copy-start(f32[4,256]{1,0:T(4,128)S(1)} %add_rsqrt_fusion) | copy-start | bytes 12292
  66.4 11.7 copy-start.11
  66.4 24.4 %copy-start.12 = (s32[4,256]{1,0:T(4,128)S(1)}, s32[4,256]{1,0:T(4,128)}, u32[]{:S(2)}) copy-start(s32[4,256]{1,0:T(4,128)} %param.12) | copy-start | bytes 12292
  101.9 143.3 %all-to-all-start = ((bf16[4,256,16,3,128]{4,1,3,0,2:T(8,128)(2,1)}), bf16[4,256,16,3,128]{4,1,3,0,2:T(8,128)(2,1)}, u32[]{:S(2)}, u32[]{:S(2)}) async-start(bf16[4,256,16,3,128]{4,1,3,0,2:T(8,128)(2,1)} %copy.65), calls=%async_computation | async-start | bytes 25165824 | tf_op jit(solution)/shard_map/all_to_all | solution.py:57
  142.1 1.9 copy-start
  582.5 77.1 %all-to-all-start.1 = ((bf16[4,2048,2,128]{3,2,0,1:T(2,128)(2,1)}), bf16[4,2048,2,128]{3,2,0,1:T(2,128)(2,1)}, u32[]{:S(2)}, u32[]{:S(2)}) async-start(bf16[4,2048,2,128]{3,2,0,1:T(2,128)(2,1)} %copy.69), calls=%async_computation.1 | async-start | bytes 8388608 | tf_op jit(solution)/shard_map/all_to_all | solution.py:69
  659.6 143.1 %all-to-all-start.3 = ((bf16[4,2048,2,3,128]{4,2,0,3,1:T(2,128)(2,1)}), bf16[4,2048,2,3,128]{4,2,0,3,1:T(2,128)(2,1)}, u32[]{:S(2)}, u32[]{:S(2)}) async-start(bf16[4,2048,2,3,128]{4,2,0,3,1:T(2,128)(2,1)} %copy.80), calls=%async_computation.3 | async-start | bytes 25165824 | tf_op jit(solution)/shard_map/all_to_all | solution.py:77
  663.7 933.9 %all-reduce.4.cloned.1.call-start = ((), (), s32[]{:S(2)}) async-start(), calls=%async_computation.4 | async-start | bytes 134217728 | tf_op jit(solution)/shard_map/psum | solution.py:84
  802.7 12.0 copy-start.2
  802.7 12.0 copy-start.5
  802.7 12.0 copy-start.8
  802.7 12.0 copy-start.10
  802.7 12.0 copy-start.14
  850.2 0.7 copy-start.15
  904.9 36.7 %copy-start.3 = (bf16[4,256,2048]{2,1,0:T(8,128)(2,1)S(1)}, bf16[4,256,2048]{2,1,0:T(8,128)(2,1)}, u32[]{:S(2)}) copy-start(bf16[4,256,2048]{2,1,0:T(8,128)(2,1)} %param.10) | copy-start | bytes 12582916
Sparse Core Ops, SparseCore 0:
  850.4 747.1 all-reduce.3
where the time goes:
time: 1670 us; the launch traced here: 1660 us
  waiting for transfers between devices  820 us (49%)
  matrix products  432 us (26%)
  local copies, waits for them, and re-layouts  199 us (12%)
  other arithmetic  133 us (8%)
  blocking collectives  48.1 us (3%)
    psum x1, waiting for transfers between devices, block_fn(): lax.psum((grad_w_qkv, grad_b_qkv, grad_w_out, grad_b_out, grad_gain, grad...  623 us
    all_to_all x1, waiting for transfers between devices, block_fn(): dqkv_loc = lax.all_to_all(dqkv_head, 'sp', 1, 2, tiled=True)  108 us
    sub x1, matrix products, attn_probs(): return jax.nn.softmax(jnp.where(allowed, scores, MASK_FILL), axis=-1)  95.8 us
    all_to_all x1, waiting for transfers between devices, block_fn(): qkv_head = lax.all_to_all(qkv_loc, 'sp', 2, 1, tiled=True)  88.5 us
    unnamed x36, local copies, waits for them, and re-layouts  69.1 us
    dot_general x1, matrix products, attn_backward(): jnp.einsum('bqnd,bknd->bnqk', do_part, v_part, preferred_element_type=jnp...  66.9 us
    convert_element_type x1, other arithmetic, block_fn(): prob_lo = attn_prob.astype(jnp.bfloat16)  64.2 us
    all_to_all x3, local copies, waits for them, and re-layouts, block_fn(): dqkv_loc = lax.all_to_all(dqkv_head, 'sp', 1, 2, tiled=True)  45 us
  transfers between devices with their start and end apart: 5, of which 3 were waited for; matrix products, arithmetic and copies ran while one was open for 18% of the time, Pallas kernels for 0%

commit v1 on v0

v1 whole, which is shorter than its diff:
```python
import functools

import jax
import jax.numpy as jnp
from jax import lax
from jax.experimental import pallas as pl
from jax.experimental.pallas import tpu as pltpu
from jax.sharding import PartitionSpec as P


NORM_EPS = 1e-5
MASK_FILL = -1e30
LOG2E = 1.4426950408889634


NT = (((1,), (1,)), ((), ()))
NN = (((1,), (0,)), ((), ()))


def dot(a, b, dims=NN):
    return lax.dot_general(a, b, dims, preferred_element_type=jnp.float32)


def stage_kernel(me_ref, slope_ref, x0_ref, x1_ref, d0_ref, d1_ref, w_ref, b_ref, wo_ref, pos_ref, *refs, nblk, blk, dim, heads, scale, first):
    if first:
        gwi_ref = gwoi_ref = None
    else:
        gwi_ref, gwoi_ref = refs[:2]
        refs = refs[2:]
    out_ref, gw_ref, gwo_ref, qkv_ref, do_ref, s_ref, dk_ref, dv_ref, kt_ref, vt_ref, ot_ref, dqp_ref, xv_ref, dv_all_ref, x_sem, d_sem = refs
    step = pl.program_id(0)
    me = me_ref[0]
    width = 3 * dim
    half = nblk // 2

    def load(b):
        p, at = b // half, pl.ds((b % half) * blk, blk)
        return (pltpu.make_async_copy((x0_ref, x1_ref)[p].at[at], xv_ref.at[b], x_sem.at[b]),
                pltpu.make_async_copy((d0_ref, d1_ref)[p].at[at], dv_all_ref.at[b], d_sem.at[b]))

    @pl.when(step == 0)
    def _():
        for b in range(nblk):
            for copy in load(b):
                copy.start()

    for b in range(nblk):
        @pl.when(step == b)
        def _(b=b):
            for copy in load(b):
                copy.wait()

    @pl.when(step < nblk)
    def _():
        at = pl.ds(pl.multiple_of(step * blk, blk), blk)
        qkv = (dot(xv_ref[step], w_ref[...]) + b_ref[...]).astype(jnp.bfloat16)
        qkv_ref[at, :] = qkv
        do_ref[at, :] = dot(dv_all_ref[step], wo_ref[...], NT).astype(jnp.bfloat16)
        for h in range(heads):
            kt_ref[h, step] = qkv[:, h * width + dim:h * width + 2 * dim].T
            vt_ref[h, step] = qkv[:, h * width + 2 * dim:(h + 1) * width].T

    @pl.when(step == 0)
    def _():
        dk_ref[...] = jnp.zeros_like(dk_ref)
        dv_ref[...] = jnp.zeros_like(dv_ref)

    @pl.when((step >= nblk) & (step < 2 * nblk))
    def _():
        attend(step - nblk, me, slope_ref, qkv_ref, do_ref, pos_ref, out_ref, s_ref, dk_ref, dv_ref, kt_ref, vt_ref, ot_ref, dqp_ref,
               nblk=nblk, blk=blk, dim=dim, heads=heads, scale=scale)

    @pl.when(step >= 2 * nblk)
    def _():
        tile = gw_ref.shape[0]
        cols = pl.ds(pl.multiple_of((step - 2 * nblk) * tile, tile), tile)
        xt = jnp.concatenate([xv_ref[b, :, cols] for b in range(nblk)], axis=0)
        gw = dot(xt.T, dqp_ref[...])
        gwo = 0.0
        for b in range(nblk):
            gwo += dot(ot_ref[b], dv_all_ref[b, :, cols])
        gw_ref[...] = gw if first else gwi_ref[...] + gw
        gwo_ref[...] = gwo if first else gwoi_ref[...] + gwo


def attend(i, me, slope_ref, qkv_ref, do_ref, pos_ref, out_ref, s_ref, dk_ref, dv_ref, kt_ref, vt_ref, ot_ref, dqp_ref,
           *, nblk, blk, dim, heads, scale):
    width = 3 * dim

    def block_of(j):
        r = jnp.bitwise_xor(j, me)
        return lax.rem(r, 2) * (nblk // 2) + lax.div(r, 2)

    def rows(j):
        return pl.ds(pl.multiple_of(block_of(j) * blk, blk), blk)

    def fold(t, op):
        return op(t.reshape(blk // 8, 8, blk), axis=0)

    qrows = rows(i)
    orows = pl.ds(pl.multiple_of(i * blk, blk), blk)
    qs = [qkv_ref[qrows, h * width:h * width + dim] for h in range(heads)]
    dos = [do_ref[qrows, h * dim:(h + 1) * dim] for h in range(heads)]
    dots = [d.T for d in dos]
    pos_first = pos_ref[pl.ds(pl.multiple_of(i * blk, blk), 8), 0:1][:1]

    def scores(j, h):
        k = qkv_ref[rows(j), h * width + dim:h * width + 2 * dim]
        lrows = pl.ds(pl.multiple_of(j * blk, blk), blk)
        bias = (pos_ref[lrows, 0:1] - pos_first) * slope_ref[h] + pos_ref[lrows, 1:2]
        return dot(k, qs[h], NT) * (scale * LOG2E) + bias

    pairs = lax.div(i, 2)
    gap = lax.broadcasted_iota(jnp.int32, (blk, blk), 0) - lax.broadcasted_iota(jnp.int32, (blk, blk), 1)

    def score_pair(m, mx, masked):
        new = list(mx)
        for t in range(2):
            j = 2 * m + t
            for h in range(heads):
                s = scores(j, h)
                if masked:
                    s = jnp.where(gap <= (i - j) * blk, s, MASK_FILL)
                s_ref[h, j] = s
                new[h] = jnp.maximum(new[h], fold(s, jnp.max))
        return tuple(new)

    start = tuple(jnp.full((8, blk), MASK_FILL, jnp.float32) for _ in range(heads))
    mx = lax.fori_loop(0, pairs, lambda m, c: score_pair(m, c, False), start)
    mx = score_pair(pairs, mx, True)
    tops = [jnp.max(v, axis=0, keepdims=True) for v in mx]

    def weigh_pair(m, carry):
        tot, acc = list(carry[0]), list(carry[1])
        for t in range(2):
            j = 2 * m + t
            for h in range(heads):
                p = jnp.exp2(s_ref[h, j] - tops[h])
                s_ref[h, j] = p
                tot[h] = tot[h] + fold(p, jnp.sum)
                acc[h] = acc[h] + dot(vt_ref[h, block_of(j)], p.astype(jnp.bfloat16))
        return tuple(tot), tuple(acc)

    zero_t = tuple(jnp.zeros((dim, blk), jnp.float32) for _ in range(heads))
    tot, ots = lax.fori_loop(0, pairs + 1, weigh_pair, (tuple(jnp.zeros((8, blk), jnp.float32) for _ in range(heads)), zero_t))
    inv = [1.0 / jnp.sum(t, axis=0, keepdims=True) for t in tot]
    rs = []
    for h in range(heads):
        o_lo = (ots[h] * inv[h]).astype(jnp.bfloat16)
        rs.append(jnp.sum(dots[h].astype(jnp.float32) * o_lo.astype(jnp.float32), axis=0, keepdims=True))
        ot_ref[block_of(i), h * dim:(h + 1) * dim, :] = o_lo
        out_ref[orows, heads * width + h * dim:heads * width + (h + 1) * dim] = o_lo.T

    def grad_pair(m, acc):
        new = list(acc)
        for t in range(2):
            jx = block_of(2 * m + t)
            for h in range(heads):
                v = qkv_ref[rows(2 * m + t), h * width + 2 * dim:(h + 1) * width]
                p = s_ref[h, 2 * m + t] * inv[h]
                ds = (p * (dot(v, dos[h], NT) - rs[h])).astype(jnp.bfloat16)
                dv_ref[h, jx] += dot(p.astype(jnp.bfloat16), dos[h])
                dk_ref[h, jx] += dot(ds, qs[h])
                new[h] = new[h] + dot(kt_ref[h, jx], ds)
        return tuple(new)

    dqts = lax.fori_loop(0, pairs + 1, grad_pair, zero_t)
    for h in range(heads):
        dq = (dqts[h] * scale).astype(jnp.bfloat16).T
        out_ref[orows, h * width:h * width + dim] = dq
        dqp_ref[qrows, h * width:h * width + dim] = dq

    @pl.when(i == nblk - 1)
    def _():
        for b in range(nblk):
            r = 2 * (b % (nblk // 2)) + b // (nblk // 2)
            lrows = pl.ds(pl.multiple_of(jnp.bitwise_xor(me, r) * blk, blk), blk)
            for h in range(heads):
                dk = (dk_ref[h, b] * scale).astype(jnp.bfloat16)
                dv = dv_ref[h, b].astype(jnp.bfloat16)
                for ref, at in ((out_ref, lrows), (dqp_ref, slice(b * blk, (b + 1) * blk))):
                    ref[at, h * width + dim:h * width + 2 * dim] = dk
                    ref[at, h * width + 2 * dim:(h + 1) * width] = dv


def stage(me, slopes, x_two, d_two, w, b, wo, pos, gw, gwo, nblk, heads, dim):
    n, hidden = x_two[0].shape
    seq = 2 * n
    blk = seq // nblk
    width, owidth = 3 * heads * dim, heads * dim
    tile = hidden // nblk
    first = gw is None
    body = functools.partial(stage_kernel, nblk=nblk, blk=blk, dim=dim, heads=heads, scale=dim ** -0.5, first=first)
    tiles = heads * nblk * (nblk + 1) // 2

    def late(i):
        return jnp.maximum(i - 2 * nblk, 0)

    def fixed(shape):
        return pl.BlockSpec(shape, lambda i, m: (0, 0), pipeline_mode=pl.Buffered(1))

    gw_spec = pl.BlockSpec((tile, width), lambda i, m: (late(i), 0))
    gwo_spec = pl.BlockSpec((owidth, tile), lambda i, m: (0, late(i)))
    args = [x_two[0], x_two[1], d_two[0], d_two[1], w, b, wo, pos]
    in_specs = [pl.BlockSpec(memory_space=pltpu.SMEM)] + [pl.BlockSpec(memory_space=pl.ANY)] * 4 + [
                fixed(w.shape), fixed(b.shape), fixed(wo.shape), fixed(pos.shape)]
    aliases = {}
    if not first:
        args += [gw, gwo]
        in_specs += [gw_spec, gwo_spec]
        aliases = {10: 1, 11: 2}
    flops = tiles * 12 * blk * blk * dim + 4 * seq * hidden * (width + owidth)
    return pl.pallas_call(
        body,
        grid_spec=pltpu.PrefetchScalarGridSpec(
            num_scalar_prefetch=1,
            grid=(3 * nblk,),
            in_specs=in_specs,
            out_specs=[pl.BlockSpec((seq, width + owidth), lambda i, m: (0, 0), pipeline_mode=pl.Buffered(1)), gw_spec, gwo_spec],
            scratch_shapes=[
                pltpu.VMEM((seq, width), jnp.bfloat16),
                pltpu.VMEM((seq, owidth), jnp.bfloat16),
                pltpu.VMEM((heads, nblk, blk, blk), jnp.float32),
                pltpu.VMEM((heads, nblk, blk, dim), jnp.float32),
                pltpu.VMEM((heads, nblk, blk, dim), jnp.float32),
                pltpu.VMEM((heads, nblk, dim, blk), jnp.bfloat16),
                pltpu.VMEM((heads, nblk, dim, blk), jnp.bfloat16),
                pltpu.VMEM((nblk, owidth, blk), jnp.bfloat16),
                pltpu.VMEM((seq, width), jnp.bfloat16),
                pltpu.VMEM((nblk, blk, hidden), jnp.bfloat16),
                pltpu.VMEM((nblk, blk, hidden), jnp.bfloat16),
                pltpu.SemaphoreType.DMA((nblk,)),
                pltpu.SemaphoreType.DMA((nblk,)),
            ],
        ),
        out_shape=[jax.ShapeDtypeStruct((seq, width + owidth), jnp.bfloat16),
                   jax.ShapeDtypeStruct((hidden, width), jnp.float32),
                   jax.ShapeDtypeStruct((owidth, hidden), jnp.float32)],
        input_output_aliases=aliases,
        compiler_params=pltpu.CompilerParams(
            dimension_semantics=("arbitrary",), vmem_limit_bytes=60 * 1024 * 1024),
        cost_estimate=pl.CostEstimate(flops=flops, bytes_accessed=seq * hidden * 8, transcendentals=tiles * blk * blk),
        name="stage",
    )(me, slopes, *args)


def place_kernel(me_ref, p0, p1, p2, p3, *refs, heads, dim, group):
    out_ref = refs[-1]
    pieces = (p0, p1, p2, p3)
    mine = lax.rem(me_ref[0], group)
    for m in range(group):
        @pl.when(mine == m)
        def _(m=m):
            for r in range(group):
                for h in range(heads):
                    for c in range(3):
                        at = (h * 3 + c) * dim
                        out_ref[:, c, (m ^ r) * heads + h, :] = pieces[r][:, at:at + dim]


def place(me, pieces, far, row, full, shape, heads, dim):
    group = len(pieces)
    n, width = pieces[0].shape
    rows = 128
    first = row // rows
    aliases = {}
    args = list(pieces)
    in_specs = [pl.BlockSpec((rows, width), lambda g, m: (g, 0))] * group
    if full is not None:
        in_specs.append(pl.BlockSpec(memory_space=pl.ANY))
        args.append(full)
        aliases = {group + 1: 0}
    return pl.pallas_call(
        functools.partial(place_kernel, heads=heads, dim=dim, group=group),
        grid_spec=pltpu.PrefetchScalarGridSpec(
            num_scalar_prefetch=1,
            grid=(n // rows,),
            in_specs=in_specs,
            out_specs=pl.BlockSpec(
                (rows, 3, group * heads, dim),
                lambda g, m: (first + g, 0, jnp.bitwise_xor(lax.div(m[0], group), far), 0)),
        ),
        out_shape=jax.ShapeDtypeStruct(shape, jnp.float32),
        input_output_aliases=aliases,
        cost_estimate=pl.CostEstimate(flops=group * n * width * 30, bytes_accessed=group * n * width * 8, transcendentals=0),
        name="place",
    )(me, *args)


def stack_kernel(me_ref, *refs):
    out_ref = refs[-1]
    for r, p_ref in enumerate(refs[:-1]):
        out_ref[jnp.bitwise_xor(me_ref[0], r)] = p_ref[...]


def stack_rows(me, pieces):
    n, width = pieces[0].shape
    rows = 32
    return pl.pallas_call(
        stack_kernel,
        grid_spec=pltpu.PrefetchScalarGridSpec(
            num_scalar_prefetch=1,
            grid=(n // rows,),
            in_specs=[pl.BlockSpec((rows, width), lambda g, m: (g, 0))] * len(pieces),
            out_specs=pl.BlockSpec((len(pieces), rows, width), lambda g, m: (0, g, 0)),
        ),
        out_shape=jax.ShapeDtypeStruct((len(pieces), n, width), jnp.float32),
        cost_estimate=pl.CostEstimate(flops=len(pieces) * n * width * 4, bytes_accessed=len(pieces) * n * width * 8, transcendentals=0),
        name="stack_rows",
    )(me, *pieces)


CHUNKS = (640, 640, 512, 256)


def after(value, *others):
    return lax.optimization_barrier((value,) + others)[0]


def solution(mesh):
    sp_size = mesh.shape["sp"]

    def swap(v, r):
        return lax.ppermute(v, "sp", [(i, i ^ r) for i in range(sp_size)])

    def gather(b):
        half = b.shape[0] // 2
        bx, by, bs = swap(b, 2), swap(b, 4), swap(b, 1)
        bd = jnp.concatenate([swap(bx[:half], 4), swap(by[half:], 2)], 0)
        return [b, bs, bx, swap(bx, 1), by, swap(by, 1), bd, swap(bd, 1)]

    def gather_halves(b):
        half = b.shape[0] // 2
        bx, by = swap(b, 2), swap(b, 4)
        mine = jnp.concatenate([b, bx, by, swap(bx[:half], 4), swap(by[half:], 2)], 0)
        return mine, swap(mine, 1)

    def block_fn(x_blk, pos_blk, keep_blk, ln_gain, ln_bias, w_qkv, b_qkv, w_out, b_out, dy_blk):
        batch_loc, seq_loc, hidden = x_blk.shape
        num_heads, head_dim = w_qkv.shape[1], w_qkv.shape[3]
        heads = num_heads // sp_size
        width = heads * 3 * head_dim
        owidth = heads * head_dim
        me = lax.axis_index("sp")
        me_arr = me.reshape(1).astype(jnp.int32)

        def stats(x):
            x_f32 = x.astype(jnp.float32)
            centered = x_f32 - jnp.mean(x_f32, axis=-1, keepdims=True)
            inv_std = lax.rsqrt(jnp.mean(centered * centered, axis=-1, keepdims=True) + NORM_EPS)
            return x_f32, centered * inv_std, inv_std

        def norm(x):
            return (stats(x)[1] * ln_gain + ln_bias).astype(jnp.bfloat16)

        x_norms = [norm(x_blk[s]) for s in range(batch_loc)]

        pk = jnp.stack([pos_blk, keep_blk])
        pk_all = jnp.stack([pk] + [swap(pk, r) for r in range(1, sp_size)])
        pk_all = pk_all[jnp.arange(sp_size) ^ me]
        pk_all = jnp.transpose(pk_all, (1, 2, 0, 3)).reshape(2, batch_loc, sp_size * seq_loc)
        pos_col = jnp.stack([pk_all[0].astype(jnp.float32), jnp.where(pk_all[1] > 0, 0.0, MASK_FILL)], axis=-1)
        head_ids = me * heads + jnp.arange(heads)
        slopes = jnp.exp2(-8.0 * (head_ids + 1).astype(jnp.float32) / num_heads) * LOG2E

        w_flat = after(w_qkv, x_norms[0]).reshape(hidden, sp_size * width)
        w_mine = lax.dynamic_slice_in_dim(w_flat, me * width, width, 1)
        b_mine = lax.dynamic_slice_in_dim(b_qkv.reshape(sp_size, width), me, 1, 0)
        wo_mine = lax.dynamic_slice_in_dim(w_out, me * owidth, owidth, 0)

        gw = gwo = None
        results, parts = [], []
        for s in range(batch_loc):
            x_two = gather_halves(x_norms[s])
            d_two = gather_halves(dy_blk[s])
            res, gw, gwo = stage(me_arr, slopes, x_two, d_two, w_mine, b_mine, wo_mine, pos_col[s], gw, gwo,
                                 sp_size, heads, head_dim)
            parts.append(lax.all_to_all(res.reshape(sp_size, seq_loc, width + owidth), "sp", 0, 0, tiled=True))
            results.append(res)
        gb_mine = sum(jnp.sum(after(d, gw)[:, :width].astype(jnp.float32), axis=0) for d in results)

        got = jnp.stack(lax.optimization_barrier((parts, gw))[0])
        got = jnp.transpose(got, (0, 2, 1, 3))
        dq_loc = got[..., :width].reshape(batch_loc, seq_loc, sp_size * width)
        o_loc = got[..., width:].reshape(batch_loc, seq_loc, hidden)
        x_f32, x_hat, inv_std = stats(after(x_blk, gw))
        y_blk = (x_f32 + jnp.einsum("bsh,hk->bsk", o_loc, w_out, preferred_element_type=jnp.float32) + b_out).astype(jnp.bfloat16)
        d_norm = jnp.einsum("bsk,hk->bsh", dq_loc, w_flat, preferred_element_type=jnp.float32)
        gg = jnp.sum(d_norm * x_hat, axis=(0, 1))
        gb = jnp.sum(d_norm, axis=(0, 1))
        e = d_norm * ln_gain
        d_ln = inv_std * (e - jnp.mean(e, axis=-1, keepdims=True) - x_hat * jnp.mean(e * x_hat, axis=-1, keepdims=True))
        grad_x = (dy_blk.astype(jnp.float32) + d_ln).astype(jnp.bfloat16)

        gbo = jnp.sum(after(dy_blk, gw).astype(jnp.float32), axis=(0, 1))
        vec = jnp.concatenate([gb_mine, gg, gb, gbo])
        vecs = jnp.stack([vec] + [swap(vec, r) for r in range(1, sp_size)])
        grad_b_qkv = vecs[:, :width][jnp.arange(sp_size) ^ me].reshape(b_qkv.shape)
        sums = jnp.sum(vecs[:, width:], axis=0)
        grad_gain, grad_bias, grad_b_out = sums[:hidden], sums[hidden:2 * hidden], sums[2 * hidden:]

        wo_pieces = gather(gwo)
        grad_w_out = stack_rows(me_arr, wo_pieces).reshape(hidden, hidden)
        grad_w_qkv = None
        group = sp_size // 2
        row = 0
        for n in CHUNKS:
            pieces = gather(gw[row:row + n])
            for far in (0, 1):
                grad_w_qkv = place(me_arr, pieces[far * group:(far + 1) * group], far, row, grad_w_qkv,
                                   (hidden, 3, num_heads, head_dim), heads, head_dim)
            row += n
        grad_w_qkv = jnp.transpose(grad_w_qkv, (0, 2, 1, 3))
        return (y_blk, grad_x, grad_w_qkv, grad_b_qkv, grad_w_out, grad_b_out, grad_gain, grad_bias)

    act_spec = P("dp", "sp", None)
    tok_spec = P("dp", "sp")
    in_specs = (act_spec, tok_spec, tok_spec, P(), P(), P(), P(), P(), P(), act_spec)
    out_specs = (act_spec, act_spec, P("dp", None, None, None), P("dp", None, None), P("dp", None), P("dp"), P("dp"), P("dp"))
    return jax.shard_map(block_fn, mesh=mesh, in_specs=in_specs, out_specs=out_specs, check_vma=False)
```

time: 1670 us -> 1310 us (0.78)
  matrix products: 432 us -> 49 us
  Pallas kernels: 0 us -> 371 us
  waiting for transfers between devices: 820 us -> 524 us
  other arithmetic: 133 us -> 33.9 us
  starting transfers between devices: 16.5 us -> 73.3 us
  local copies, waits for them, and re-layouts: 199 us -> 143 us
  blocking collectives: 48.1 us -> 104 us
    psum x1 -> x0, waiting for transfers between devices: 623 us -> none  [block_fn(): lax.psum((grad_w_qkv, grad_b_qkv, grad_w_out, grad_b_out, grad_gain, grad...]
    ppermute x0 -> x94, waiting for transfers between devices: none -> 524 us  [swap(): return lax.ppermute(v, 'sp', [(i, i ^ r) for i in range(sp_size)])]
    pallas_call x0 -> x13, Pallas kernels: none -> 371 us  [the longest x4 295 us: stage(): pl.pallas_call(body, grid_spec=pltpu.PrefetchScalarGridSpec(num_scalar_pr...]
    dot_general x10 -> x1, matrix products: 321 us -> 36.3 us  [block_fn(): jnp.einsum('bsk,hk->bsh', dq_loc, w_flat, preferred_element_type=jnp.floa...]
    all_to_all x4 -> x2, waiting for transfers between devices: 197 us -> 0.01 us  [block_fn(): lax.all_to_all(res.reshape(sp_size, seq_loc, width + owidth), 'sp', 0, 0,...]
    all_to_all x0 -> x2, blocking collectives: none -> 104 us  [block_fn(): lax.all_to_all(res.reshape(sp_size, seq_loc, width + owidth), 'sp', 0, 0,...]
    sub x1 -> x0, matrix products: 95.8 us -> none  [attn_probs(): return jax.nn.softmax(jnp.where(allowed, scores, MASK_FILL), axis=-1)]
    convert_element_type x2, other arithmetic: 85.4 us -> 4.76 us  [the longest x1 4.76 us: block_fn(): grad_x = (dy_blk.astype(jnp.float32) + d_ln).astype(jnp.bfloat16)]
  transfers between devices with their start and end apart: 5 -> 96, of which waited for: 3 -> 33; matrix products, arithmetic and copies ran while one was open for 18% -> 16% of each run, Pallas kernels for 0% -> 22%
where the time goes in v1:
time: 1310 us; the launch traced here: 1300 us
  waiting for transfers between devices  524 us (40%)
  Pallas kernels  371 us (28%)
  local copies, waits for them, and re-layouts  143 us (11%)
  blocking collectives  104 us (8%)
  starting transfers between devices  73.3 us (6%)
  matrix products  49 us (4%)
  other arithmetic  33.9 us (3%)
    ppermute x94, waiting for transfers between devices, swap(): return lax.ppermute(v, 'sp', [(i, i ^ r) for i in range(sp_size)])  524 us
    pallas_call x4, Pallas kernels, stage(): pl.pallas_call(body, grid_spec=pltpu.PrefetchScalarGridSpec(num_scalar_pr...  295 us
    all_to_all x2, blocking collectives, block_fn(): lax.all_to_all(res.reshape(sp_size, seq_loc, width + owidth), 'sp', 0, 0,...  104 us
    ppermute x94, starting transfers between devices, swap(): return lax.ppermute(v, 'sp', [(i, i ^ r) for i in range(sp_size)])  66.4 us
    pallas_call x8, Pallas kernels, place(): pl.pallas_call(functools.partial(place_kernel, heads=heads, dim=dim, grou...  62.5 us
    unnamed x163, local copies, waits for them, and re-layouts  52.2 us
    dot_general x1, matrix products, block_fn(): jnp.einsum('bsk,hk->bsh', dq_loc, w_flat, preferred_element_type=jnp.floa...  36.3 us
    optimization_barrier x1, local copies, waits for them, and re-layouts, after(): return lax.optimization_barrier((value,) + others)[0]  33.7 us
  transfers between devices with their start and end apart: 96, of which 33 were waited for; matrix products, arithmetic and copies ran while one was open for 16% of the time, Pallas kernels for 22%

profile of v1, /device:TPU:0, one launch (start us, length us, event | category | flops | bytes accessed | tf_op | source)
XLA Modules:
  0.0 1300.1 jit_solution(749540451861495577)
XLA Ops:
  20.8 33.7 %copy.47 = bf16[2048,16,3,128]{0,3,2,1:T(8,128)(2,1)} copy(bf16[2048,16,3,128]{3,1,2,0:T(8,128)(2,1)} %param.15) | data formatting | bytes 50331648 | tf_op jit(solution)/shard_map/optimization_barrier | solution.py:317
  81.8 11.9 collective-permute-done.42
  98.3 17.8 %collective-permute-done.27 = bf16[256,2048]{1,0:T(8,128)(2,1)S(1)} collective-permute-done((bf16[256,2048]{1,0:T(8,128)(2,1)}, bf16[256,2048]{1,0:T(8,128)(2,1)S(1)}, u32[]{:S(2)}, u32[]{:S(2)}) %collective-permute-start.27) | collective-permute-done | bytes 1048608 | tf_op jit(solution)/shard_map/ppermute | solution.py:324
  120.5 18.1 %collective-permute-done.32 = bf16[256,2048]{1,0:T(8,128)(2,1)} collective-permute-done((bf16[256,2048]{1,0:T(8,128)(2,1)}, bf16[256,2048]{1,0:T(8,128)(2,1)}, u32[]{:S(2)}, u32[]{:S(2)}) %collective-permute-start.32) | collective-permute-done | bytes 1048608 | tf_op jit(solution)/shard_map/ppermute | solution.py:324
  145.0 16.1 %collective-permute-done.17 = bf16[256,2048]{1,0:T(8,128)(2,1)S(1)} collective-permute-done((bf16[256,2048]{1,0:T(8,128)(2,1)}, bf16[256,2048]{1,0:T(8,128)(2,1)S(1)}, u32[]{:S(2)}, u32[]{:S(2)}) %collective-permute-start.17) | collective-permute-done | bytes 1048608 | tf_op jit(solution)/shard_map/ppermute | solution.py:324
  167.6 15.9 %collective-permute-done.22 = bf16[256,2048]{1,0:T(8,128)(2,1)S(1)} collective-permute-done((bf16[256,2048]{1,0:T(8,128)(2,1)S(1)}, bf16[256,2048]{1,0:T(8,128)(2,1)S(1)}, u32[]{:S(2)}, u32[]{:S(2)}) %collective-permute-start.22) | collective-permute-done | bytes 1048608 | tf_op jit(solution)/shard_map/ppermute | solution.py:324
  185.8 10.7 collective-permute-done.39
  208.5 41.8 %collective-permute-done.45 = bf16[128,2048]{1,0:T(8,128)(2,1)S(1)} collective-permute-done((bf16[128,2048]{1,0:T(8,128)(2,1)S(1)}, bf16[128,2048]{1,0:T(8,128)(2,1)S(1)}, u32[]{:S(2)}, u32[]{:S(2)}) %collective-permute-start.45) | collective-permute-done | bytes 524320 | tf_op jit(solution)/shard_map/ppermute | solution.py:324
  314.4 10.4 collective-permute-done.7
  343.1 73.4 %stage.4 = (bf16[2048,1024]{1,0:T(8,128)(2,1)}, f32[2048,768]{1,0:T(8,128)}, f32[256,2048]{1,0:T(8,128)}) custom-call(s32[1]{0:T(128)} %bitcast.me_ref, f32[2]{0:T(128)} %exponential_multiply_fusion.slope_ref, bf16[1024,2048]{1,0:T(8,128)(2,1)} %copy-done.43, bf16[1024,2048]{1,0:T(8,128)(2,1)} %copy-done.56, bf16[1024,2048]{1,0:T(8,128)(2,1)} %copy-done.45, ...), custom_call_target="tpu_custom_call" | custom-call | flops 24427626496 | bytes 33554432 | tf_op jit(solution)/shard_map/stage/pallas_call | solution.py:213
  417.0 73.8 %stage.5 = (bf16[2048,1024]{1,0:T(8,128)(2,1)}, f32[2048,768]{1,0:T(8,128)}, f32[256,2048]{1,0:T(8,128)}) custom-call(s32[1]{0:T(128)} %bitcast.me_ref, f32[2]{0:T(128)} %exponential_multiply_fusion.slope_ref, bf16[1024,2048]{1,0:T(8,128)(2,1)} %constant_dynamic-update-slice_fusion.28.x0_ref, ...), custom_call_target="tpu_custom_call", output_to_operand_aliasing={{1}: (10, {}), {2}: (11, {})} | custom-call | flops 24427626496 | bytes 33554432 | tf_op jit(solution)/shard_map/stage/pallas_call | solution.py:213
  490.8 74.0 %stage.6 = (bf16[2048,1024]{1,0:T(8,128)(2,1)}, f32[2048,768]{1,0:T(8,128)}, f32[256,2048]{1,0:T(8,128)}) custom-call(s32[1]{0:T(128)} %bitcast.me_ref, f32[2]{0:T(128)} %exponential_multiply_fusion.slope_ref, bf16[1024,2048]{1,0:T(8,128)(2,1)} %constant_dynamic-update-slice_fusion.18.x0_ref, ...), custom_call_target="tpu_custom_call", output_to_operand_aliasing={{1}: (10, {}), {2}: (11, {})} | custom-call | flops 24427626496 | bytes 33554432 | tf_op jit(solution)/shard_map/stage/pallas_call | solution.py:213
  564.8 73.8 %stage.7 = (bf16[2048,1024]{1,0:T(8,128)(2,1)}, f32[2048,768]{1,0:T(8,128)}, f32[256,2048]{1,0:T(8,128)}) custom-call(s32[1]{0:T(128)} %bitcast.me_ref, f32[2]{0:T(128)} %exponential_multiply_fusion.slope_ref, bf16[1024,2048]{1,0:T(8,128)(2,1)} %constant_dynamic-update-slice_fusion.x0_ref, ...), custom_call_target="tpu_custom_call", output_to_operand_aliasing={{1}: (10, {}), {2}: (11, {})} | custom-call | flops 24427626496 | bytes 33554432 | tf_op jit(solution)/shard_map/stage/pallas_call | solution.py:213
  638.6 52.8 %all_to_all.20 = bf16[8,256,1024]{2,1,0:T(8,128)(2,1)} all-to-all(bf16[8,256,1024]{2,1,0:T(8,128)(2,1)} %bitcast.150), channel_id=1, replica_groups=mesh['dp'=1,'sp'=8] {'sp'}, dimensions={0} | all-to-all | bytes 8388608 | tf_op jit(solution)/shard_map/all_to_all | solution.py:378
  691.4 51.0 %all_to_all.21 = bf16[8,256,1024]{2,1,0:T(8,128)(2,1)} all-to-all(bf16[8,256,1024]{2,1,0:T(8,128)(2,1)S(1)} %bitcast.149), channel_id=1, replica_groups=mesh['dp'=1,'sp'=8] {'sp'}, dimensions={0} | all-to-all | bytes 8388608 | tf_op jit(solution)/shard_map/all_to_all | solution.py:378
  758.6 95.0 %collective-permute-done.49.p2 = f32[256,768]{1,0:T(8,128)} collective-permute-done((f32[256,768]{1,0:T(8,128)}, f32[256,768]{1,0:T(8,128)}, u32[]{:S(2)}, u32[]{:S(2)}) %collective-permute-start.49) | collective-permute-done | bytes 786464 | tf_op jit(solution)/shard_map/ppermute | solution.py:324
  863.0 96.3 %collective-permute-done.47.p0 = f32[256,768]{1,0:T(8,128)S(1)} collective-permute-done((f32[256,768]{1,0:T(8,128)}, f32[256,768]{1,0:T(8,128)S(1)}, u32[]{:S(2)}, u32[]{:S(2)}) %collective-permute-start.47) | collective-permute-done | bytes 786464 | tf_op jit(solution)/shard_map/ppermute | solution.py:324
  973.4 73.9 %collective-permute-done.65.p2 = f32[640,768]{1,0:T(8,128)S(1)} collective-permute-done((f32[640,768]{1,0:T(8,128)S(1)}, f32[640,768]{1,0:T(8,128)S(1)}, u32[]{:S(2)}, u32[]{:S(2)}) %collective-permute-start.65) | collective-permute-done | bytes 1966112 | tf_op jit(solution)/shard_map/ppermute | solution.py:324
  1097.7 11.6 collective-permute-done.74
  1118.8 10.6 collective-permute-done.66
  1140.0 36.3 %fusion.10 = (f32[2048]{0:T(1024)S(1)}, f32[4,256]{1,0:T(4,128)}, f32[4,256]{1,0:T(4,128)}, f32[2048]{0:T(1024)S(1)}, f32[4,256,2048]{2,1,0:T(8,128)S(1)}) fusion(bf16[4,256,2048]{2,1,0:T(8,128)(2,1)S(1)} %copy-done.2, f32[4,256]{1,0:T(4,128)} %add_rsqrt_fusion, f32[4,256]{1,0:T(4,128)S(1)} %broadcast_multiply_fusion.2, f32[2048]{0:T(1024)} %param.13, ...), kind=kOutput, calls=%fused_computation.17 | convolution fusion | flops 25790769152 | bytes 50372608 | tf_op jit(solution)/shard_map/bsk,hk->bsh/dot_general | solution.py:388
  1203.4 12.7 fusion.13
  1233.3 9.8 place.9.refs_0_
  1286.3 13.5 %stack_rows.1 = f32[8,256,2048]{2,1,0:T(8,128)} custom-call(s32[1]{0:T(128)} %bitcast.me_ref, f32[256,2048]{1,0:T(8,128)} %get-tuple-element.53.refs_0_, f32[256,2048]{1,0:T(8,128)} %collective-permute-done.86.refs_1_, f32[256,2048]{1,0:T(8,128)} %collective-permute-done.87.refs_2_, f32[256,2048]{1,0:T(8,128)} %collective-permute-done.88.refs_3_, ...), custom_call_target="tpu_custom_call" | custom-call | flops 16777216 | bytes 33554432 | tf_op jit(solution)/shard_map/stack_rows/pallas_call | solution.py:299
  (446 shorter events, 363.1 us)
Async XLA Ops:
  253.4 85.8 %collective-permute-start.41 = (bf16[1024,2048]{1,0:T(8,128)(2,1)S(1)}, bf16[1024,2048]{1,0:T(8,128)(2,1)S(1)}, u32[]{:S(2)}, u32[]{:S(2)}) collective-permute-start(bf16[1024,2048]{1,0:T(8,128)(2,1)S(1)} %constant_dynamic-update-slice_fusion.38.x0_ref), channel_id=1, source_target_pairs={{0,1},{1,0},{2,3},{3,2},{4,5},{5,4},{6,7},{7,6}} | collective-permute-start | bytes 12582920 | tf_op jit(solution)/shard_map/ppermute | solution.py:324
  253.4 86.3 %collective-permute-start.46 = (bf16[1024,2048]{1,0:T(8,128)(2,1)S(1)}, bf16[1024,2048]{1,0:T(8,128)(2,1)S(1)}, u32[]{:S(2)}, u32[]{:S(2)}) collective-permute-start(bf16[1024,2048]{1,0:T(8,128)(2,1)S(1)} %constant_dynamic-update-slice_fusion.43.d0_ref), channel_id=1, source_target_pairs={{0,1},{1,0},{2,3},{3,2},{4,5},{5,4},{6,7},{7,6}} | collective-permute-start | bytes 12582920 | tf_op jit(solution)/shard_map/ppermute | solution.py:324
  300.6 115.8 %collective-permute-start.31 = (bf16[1024,2048]{1,0:T(8,128)(2,1)}, bf16[1024,2048]{1,0:T(8,128)(2,1)}, u32[]{:S(2)}, u32[]{:S(2)}) collective-permute-start(bf16[1024,2048]{1,0:T(8,128)(2,1)} %constant_dynamic-update-slice_fusion.28.x0_ref), channel_id=1, source_target_pairs={{0,1},{1,0},{2,3},{3,2},{4,5},{5,4},{6,7},{7,6}} | collective-permute-start | bytes 12582920 | tf_op jit(solution)/shard_map/ppermute | solution.py:324
  308.5 108.5 %collective-permute-start.36 = (bf16[1024,2048]{1,0:T(8,128)(2,1)}, bf16[1024,2048]{1,0:T(8,128)(2,1)}, u32[]{:S(2)}, u32[]{:S(2)}) collective-permute-start(bf16[1024,2048]{1,0:T(8,128)(2,1)} %constant_dynamic-update-slice_fusion.33.d0_ref), channel_id=1, source_target_pairs={{0,1},{1,0},{2,3},{3,2},{4,5},{5,4},{6,7},{7,6}} | collective-permute-start | bytes 12582920 | tf_op jit(solution)/shard_map/ppermute | solution.py:324
  338.3 152.5 %collective-permute-start.21 = (bf16[1024,2048]{1,0:T(8,128)(2,1)}, bf16[1024,2048]{1,0:T(8,128)(2,1)}, u32[]{:S(2)}, u32[]{:S(2)}) collective-permute-start(bf16[1024,2048]{1,0:T(8,128)(2,1)} %constant_dynamic-update-slice_fusion.18.x0_ref), channel_id=1, source_target_pairs={{0,1},{1,0},{2,3},{3,2},{4,5},{5,4},{6,7},{7,6}} | collective-permute-start | bytes 12582920 | tf_op jit(solution)/shard_map/ppermute | solution.py:324
  339.2 151.6 %collective-permute-start.26 = (bf16[1024,2048]{1,0:T(8,128)(2,1)}, bf16[1024,2048]{1,0:T(8,128)(2,1)}, u32[]{:S(2)}, u32[]{:S(2)}) collective-permute-start(bf16[1024,2048]{1,0:T(8,128)(2,1)} %constant_dynamic-update-slice_fusion.23.d0_ref), channel_id=1, source_target_pairs={{0,1},{1,0},{2,3},{3,2},{4,5},{5,4},{6,7},{7,6}} | collective-permute-start | bytes 12582920 | tf_op jit(solution)/shard_map/ppermute | solution.py:324
  341.1 223.6 %collective-permute-start.4 = (bf16[1024,2048]{1,0:T(8,128)(2,1)}, bf16[1024,2048]{1,0:T(8,128)(2,1)}, u32[]{:S(2)}, u32[]{:S(2)}) collective-permute-start(bf16[1024,2048]{1,0:T(8,128)(2,1)} %constant_dynamic-update-slice_fusion.x0_ref), channel_id=1, source_target_pairs={{0,1},{1,0},{2,3},{3,2},{4,5},{5,4},{6,7},{7,6}} | collective-permute-start | bytes 12582920 | tf_op jit(solution)/shard_map/ppermute | solution.py:324
  416.5 148.3 %collective-permute-start.9 = (bf16[1024,2048]{1,0:T(8,128)(2,1)}, bf16[1024,2048]{1,0:T(8,128)(2,1)}, u32[]{:S(2)}, u32[]{:S(2)}) collective-permute-start(bf16[1024,2048]{1,0:T(8,128)(2,1)} %constant_dynamic-update-slice_fusion.5.d0_ref), channel_id=1, source_target_pairs={{0,1},{1,0},{2,3},{3,2},{4,5},{5,4},{6,7},{7,6}} | collective-permute-start | bytes 12582920 | tf_op jit(solution)/shard_map/ppermute | solution.py:324
  742.5 112.6 %all-to-all-start.1 = ((bf16[8,256,1024]{2,1,0:T(8,128)(2,1)}), bf16[8,256,1024]{2,1,0:T(8,128)(2,1)}, u32[]{:S(2)}, u32[]{:S(2)}) async-start(bf16[8,256,1024]{2,1,0:T(8,128)(2,1)} %bitcast.148), calls=%async_computation.1 | async-start | bytes 8388608 | tf_op jit(solution)/shard_map/all_to_all | solution.py:378
  749.5 213.3 %collective-permute-start.73 = (f32[640,768]{1,0:T(8,128)}, f32[640,768]{1,0:T(8,128)}, u32[]{:S(2)}, u32[]{:S(2)}) collective-permute-start(f32[640,768]{1,0:T(8,128)} %get-tuple-element.98.p0), channel_id=1, source_target_pairs={{0,2},{1,3},{2,0},{3,1},{4,6},{5,7},{6,4},{7,5}} | collective-permute-start | bytes 5898248 | tf_op jit(solution)/shard_map/ppermute | solution.py:324
  753.5 100.1 %collective-permute-start.49 = (f32[256,768]{1,0:T(8,128)}, f32[256,768]{1,0:T(8,128)}, u32[]{:S(2)}, u32[]{:S(2)}) collective-permute-start(f32[256,768]{1,0:T(8,128)} %slice.199.p0), channel_id=1, source_target_pairs={{0,2},{1,3},{2,0},{3,1},{4,6},{5,7},{6,4},{7,5}} | collective-permute-start | bytes 2359304 | tf_op jit(solution)/shard_map/ppermute | solution.py:324
  754.2 104.4 %collective-permute-start.53 = (f32[256,768]{1,0:T(8,128)}, f32[256,768]{1,0:T(8,128)}, u32[]{:S(2)}, u32[]{:S(2)}) collective-permute-start(f32[256,768]{1,0:T(8,128)} %slice.199.p0), channel_id=1, source_target_pairs={{0,1},{1,0},{2,3},{3,2},{4,5},{5,4},{6,7},{7,6}} | collective-permute-start | bytes 2359304 | tf_op jit(solution)/shard_map/ppermute | solution.py:324
  755.7 204.2 %collective-permute-start.57 = (f32[512,768]{1,0:T(8,128)S(1)}, f32[512,768]{1,0:T(8,128)}, u32[]{:S(2)}, u32[]{:S(2)}) collective-permute-start(f32[512,768]{1,0:T(8,128)S(1)} %slice.202.p0), channel_id=1, source_target_pairs={{0,2},{1,3},{2,0},{3,1},{4,6},{5,7},{6,4},{7,5}} | collective-permute-start | bytes 4718600 | tf_op jit(solution)/shard_map/ppermute | solution.py:324
  757.1 204.3 %collective-permute-start.55 = (f32[512,768]{1,0:T(8,128)S(1)}, f32[512,768]{1,0:T(8,128)}, u32[]{:S(2)}, u32[]{:S(2)}) collective-permute-start(f32[512,768]{1,0:T(8,128)S(1)} %slice.202.p0), channel_id=1, source_target_pairs={{0,4},{1,5},{2,6},{3,7},{4,0},{5,1},{6,2},{7,3}} | collective-permute-start | bytes 4718600 | tf_op jit(solution)/shard_map/ppermute | solution.py:324
  853.6 115.4 %collective-permute-start.71 = (f32[640,768]{1,0:T(8,128)}, f32[640,768]{1,0:T(8,128)}, u32[]{:S(2)}, u32[]{:S(2)}) collective-permute-start(f32[640,768]{1,0:T(8,128)} %get-tuple-element.98.p0), channel_id=1, source_target_pairs={{0,4},{1,5},{2,6},{3,7},{4,0},{5,1},{6,2},{7,3}} | collective-permute-start | bytes 5898248 | tf_op jit(solution)/shard_map/ppermute | solution.py:324
  855.1 212.0 %all-to-all-start = ((bf16[8,256,1024]{2,1,0:T(8,128)(2,1)}), bf16[8,256,1024]{2,1,0:T(8,128)(2,1)}, u32[]{:S(2)}, u32[]{:S(2)}) async-start(bf16[8,256,1024]{2,1,0:T(8,128)(2,1)} %bitcast.147), calls=%async_computation | async-start | bytes 8388608 | tf_op jit(solution)/shard_map/all_to_all | solution.py:378
  858.6 100.7 %collective-permute-start.47 = (f32[256,768]{1,0:T(8,128)}, f32[256,768]{1,0:T(8,128)S(1)}, u32[]{:S(2)}, u32[]{:S(2)}) collective-permute-start(f32[256,768]{1,0:T(8,128)} %slice.199.p0), channel_id=1, source_target_pairs={{0,4},{1,5},{2,6},{3,7},{4,0},{5,1},{6,2},{7,3}} | collective-permute-start | bytes 2359304 | tf_op jit(solution)/shard_map/ppermute | solution.py:324
  959.3 89.1 %collective-permute-start.87 = (f32[256,2048]{1,0:T(8,128)}, f32[256,2048]{1,0:T(8,128)}, u32[]{:S(2)}, u32[]{:S(2)}) collective-permute-start(f32[256,2048]{1,0:T(8,128)} %get-tuple-element.53.refs_0_), channel_id=1, source_target_pairs={{0,2},{1,3},{2,0},{3,1},{4,6},{5,7},{6,4},{7,5}} | collective-permute-start | bytes 6291464 | tf_op jit(solution)/shard_map/ppermute | solution.py:324
  960.0 89.3 %collective-permute-start.89 = (f32[256,2048]{1,0:T(8,128)}, f32[256,2048]{1,0:T(8,128)}, u32[]{:S(2)}, u32[]{:S(2)}) collective-permute-start(f32[256,2048]{1,0:T(8,128)} %get-tuple-element.53.refs_0_), channel_id=1, source_target_pairs={{0,4},{1,5},{2,6},{3,7},{4,0},{5,1},{6,2},{7,3}} | collective-permute-start | bytes 6291464 | tf_op jit(solution)/shard_map/ppermute | solution.py:324
  961.3 86.0 %collective-permute-start.65 = (f32[640,768]{1,0:T(8,128)S(1)}, f32[640,768]{1,0:T(8,128)S(1)}, u32[]{:S(2)}, u32[]{:S(2)}) collective-permute-start(f32[640,768]{1,0:T(8,128)S(1)} %get-tuple-element.99.p0), channel_id=1, source_target_pairs={{0,2},{1,3},{2,0},{3,1},{4,6},{5,7},{6,4},{7,5}} | collective-permute-start | bytes 5898248 | tf_op jit(solution)/shard_map/ppermute | solution.py:324
  962.8 85.5 %collective-permute-start.63 = (f32[640,768]{1,0:T(8,128)S(1)}, f32[640,768]{1,0:T(8,128)S(1)}, u32[]{:S(2)}, u32[]{:S(2)}) collective-permute-start(f32[640,768]{1,0:T(8,128)S(1)} %get-tuple-element.99.p0), channel_id=1, source_target_pairs={{0,4},{1,5},{2,6},{3,7},{4,0},{5,1},{6,2},{7,3}} | collective-permute-start | bytes 5898248 | tf_op jit(solution)/shard_map/ppermute | solution.py:324
  968.9 98.7 %collective-permute-start.61 = (f32[512,768]{1,0:T(8,128)S(1)}, f32[512,768]{1,0:T(8,128)}, u32[]{:S(2)}, u32[]{:S(2)}) collective-permute-start(f32[512,768]{1,0:T(8,128)S(1)} %slice.202.p0), channel_id=1, source_target_pairs={{0,1},{1,0},{2,3},{3,2},{4,5},{5,4},{6,7},{7,6}} | collective-permute-start | bytes 4718600 | tf_op jit(solution)/shard_map/ppermute | solution.py:324
  1202.0 84.3 %collective-permute-start.86 = (f32[256,2048]{1,0:T(8,128)}, f32[256,2048]{1,0:T(8,128)}, u32[]{:S(2)}, u32[]{:S(2)}) collective-permute-start(f32[256,2048]{1,0:T(8,128)} %get-tuple-element.53.refs_0_), channel_id=1, source_target_pairs={{0,1},{1,0},{2,3},{3,2},{4,5},{5,4},{6,7},{7,6}} | collective-permute-start | bytes 6291464 | tf_op jit(solution)/shard_map/ppermute | solution.py:324
  1202.3 84.0 %collective-permute-start.88 = (f32[256,2048]{1,0:T(8,128)}, f32[256,2048]{1,0:T(8,128)}, u32[]{:S(2)}, u32[]{:S(2)}) collective-permute-start(f32[256,2048]{1,0:T(8,128)} %collective-permute-done.87.refs_2_), channel_id=1, source_target_pairs={{0,1},{1,0},{2,3},{3,2},{4,5},{5,4},{6,7},{7,6}} | collective-permute-start | bytes 6291464 | tf_op jit(solution)/shard_map/ppermute | solution.py:324
  (131 other events, 4040.4 us)

commit v2 on v1

--- a/solution.py
+++ b/solution.py
@@ -27,7 +27,7 @@
     else:
         gwi_ref, gwoi_ref = refs[:2]
         refs = refs[2:]
-    out_ref, gw_ref, gwo_ref, qkv_ref, do_ref, s_ref, dk_ref, dv_ref, kt_ref, vt_ref, ot_ref, dqp_ref, xv_ref, dv_all_ref, x_sem, d_sem = refs
+    out_ref, gw_ref, gwo_ref, qkv_ref, do_ref, s_ref, dk_ref, dv_ref, kt_ref, vt_ref, ot_ref, xv_ref, dv_all_ref, x_sem, d_sem = refs
     step = pl.program_id(0)
     me = me_ref[0]
     width = 3 * dim
@@ -52,141 +52,130 @@
 
     @pl.when(step < nblk)
     def _():
-        at = pl.ds(pl.multiple_of(step * blk, blk), blk)
+        tok = jnp.bitwise_xor(me, 2 * lax.rem(step, half) + lax.div(step, half))
+        pair, side = lax.div(tok, 2), lax.rem(tok, 2)
+        at = pl.ds(pl.multiple_of(tok * blk, blk), blk)
         qkv = (dot(xv_ref[step], w_ref[...]) + b_ref[...]).astype(jnp.bfloat16)
         qkv_ref[at, :] = qkv
         do_ref[at, :] = dot(dv_all_ref[step], wo_ref[...], NT).astype(jnp.bfloat16)
         for h in range(heads):
-            kt_ref[h, step] = qkv[:, h * width + dim:h * width + 2 * dim].T
-            vt_ref[h, step] = qkv[:, h * width + 2 * dim:(h + 1) * width].T
+            lanes = pl.ds(pl.multiple_of(side * blk, blk), blk)
+            kt_ref[h, pair, :, lanes] = qkv[:, h * width + dim:h * width + 2 * dim].T
+            vt_ref[h, pair, :, lanes] = qkv[:, h * width + 2 * dim:(h + 1) * width].T
 
     @pl.when(step == 0)
     def _():
         dk_ref[...] = jnp.zeros_like(dk_ref)
         dv_ref[...] = jnp.zeros_like(dv_ref)
 
-    @pl.when((step >= nblk) & (step < 2 * nblk))
-    def _():
-        attend(step - nblk, me, slope_ref, qkv_ref, do_ref, pos_ref, out_ref, s_ref, dk_ref, dv_ref, kt_ref, vt_ref, ot_ref, dqp_ref,
+    @pl.when((step >= nblk) & (step < nblk + half))
+    def _():
+        attend(step - nblk, slope_ref, qkv_ref, do_ref, pos_ref, out_ref, s_ref, dk_ref, dv_ref, kt_ref, vt_ref, ot_ref,
                nblk=nblk, blk=blk, dim=dim, heads=heads, scale=scale)
 
-    @pl.when(step >= 2 * nblk)
+    @pl.when(step >= nblk + half)
     def _():
         tile = gw_ref.shape[0]
-        cols = pl.ds(pl.multiple_of((step - 2 * nblk) * tile, tile), tile)
-        xt = jnp.concatenate([xv_ref[b, :, cols] for b in range(nblk)], axis=0)
-        gw = dot(xt.T, dqp_ref[...])
+        cols = pl.ds(pl.multiple_of((step - nblk - half) * tile, tile), tile)
+        places = []
+        for j in range(nblk):
+            r = jnp.bitwise_xor(me, j)
+            places.append(lax.rem(r, 2) * half + lax.div(r, 2))
+        xt = jnp.concatenate([xv_ref[p, :, cols] for p in places], axis=0)
+        gw = dot(xt.T, out_ref[:, :heads * width])
         gwo = 0.0
-        for b in range(nblk):
-            gwo += dot(ot_ref[b], dv_all_ref[b, :, cols])
+        for j, p in enumerate(places):
+            gwo += dot(ot_ref[j // 2, :, (j % 2) * blk:(j % 2 + 1) * blk], dv_all_ref[p, :, cols])
         gw_ref[...] = gw if first else gwi_ref[...] + gw
         gwo_ref[...] = gwo if first else gwoi_ref[...] + gwo
 
 
-def attend(i, me, slope_ref, qkv_ref, do_ref, pos_ref, out_ref, s_ref, dk_ref, dv_ref, kt_ref, vt_ref, ot_ref, dqp_ref,
+def attend(i, slope_ref, qkv_ref, do_ref, pos_ref, out_ref, s_ref, dk_ref, dv_ref, kt_ref, vt_ref, ot_ref,
            *, nblk, blk, dim, heads, scale):
     width = 3 * dim
-
-    def block_of(j):
-        r = jnp.bitwise_xor(j, me)
-        return lax.rem(r, 2) * (nblk // 2) + lax.div(r, 2)
-
-    def rows(j):
-        return pl.ds(pl.multiple_of(block_of(j) * blk, blk), blk)
+    big = 2 * blk
+
+    def rows(m):
+        return pl.ds(pl.multiple_of(m * big, big), big)
 
     def fold(t, op):
-        return op(t.reshape(blk // 8, 8, blk), axis=0)
+        return op(t.reshape(big // 8, 8, big), axis=0)
 
     qrows = rows(i)
-    orows = pl.ds(pl.multiple_of(i * blk, blk), blk)
     qs = [qkv_ref[qrows, h * width:h * width + dim] for h in range(heads)]
     dos = [do_ref[qrows, h * dim:(h + 1) * dim] for h in range(heads)]
     dots = [d.T for d in dos]
-    pos_first = pos_ref[pl.ds(pl.multiple_of(i * blk, blk), 8), 0:1][:1]
-
-    def scores(j, h):
-        k = qkv_ref[rows(j), h * width + dim:h * width + 2 * dim]
-        lrows = pl.ds(pl.multiple_of(j * blk, blk), blk)
-        bias = (pos_ref[lrows, 0:1] - pos_first) * slope_ref[h] + pos_ref[lrows, 1:2]
+    pos_first = pos_ref[pl.ds(pl.multiple_of(i * big, big), 8), 0:1][:1]
+
+    def scores(m, h):
+        k = qkv_ref[rows(m), h * width + dim:h * width + 2 * dim]
+        bias = (pos_ref[rows(m), 0:1] - pos_first) * slope_ref[h] + pos_ref[rows(m), 1:2]
         return dot(k, qs[h], NT) * (scale * LOG2E) + bias
 
-    pairs = lax.div(i, 2)
-    gap = lax.broadcasted_iota(jnp.int32, (blk, blk), 0) - lax.broadcasted_iota(jnp.int32, (blk, blk), 1)
-
     def score_pair(m, mx, masked):
-        new = list(mx)
-        for t in range(2):
-            j = 2 * m + t
-            for h in range(heads):
-                s = scores(j, h)
-                if masked:
-                    s = jnp.where(gap <= (i - j) * blk, s, MASK_FILL)
-                s_ref[h, j] = s
-                new[h] = jnp.maximum(new[h], fold(s, jnp.max))
+        new = []
+        for h in range(heads):
+            s = scores(m, h)
+            if masked:
+                seen = lax.broadcasted_iota(jnp.int32, (big, big), 0) <= lax.broadcasted_iota(jnp.int32, (big, big), 1)
+                s = jnp.where(seen, s, MASK_FILL)
+            s_ref[h, m] = s
+            new.append(jnp.maximum(mx[h], fold(s, jnp.max)))
         return tuple(new)
 
-    start = tuple(jnp.full((8, blk), MASK_FILL, jnp.float32) for _ in range(heads))
-    mx = lax.fori_loop(0, pairs, lambda m, c: score_pair(m, c, False), start)
-    mx = score_pair(pairs, mx, True)
+    start = tuple(jnp.full((8, big), MASK_FILL, jnp.float32) for _ in range(heads))
+    mx = lax.fori_loop(0, i, lambda m, c: score_pair(m, c, False), start)
+    mx = score_pair(i, mx, True)
     tops = [jnp.max(v, axis=0, keepdims=True) for v in mx]
 
     def weigh_pair(m, carry):
-        tot, acc = list(carry[0]), list(carry[1])
-        for t in range(2):
-            j = 2 * m + t
-            for h in range(heads):
-                p = jnp.exp2(s_ref[h, j] - tops[h])
-                s_ref[h, j] = p
-                tot[h] = tot[h] + fold(p, jnp.sum)
-                acc[h] = acc[h] + dot(vt_ref[h, block_of(j)], p.astype(jnp.bfloat16))
+        tot, acc = [], []
+        for h in range(heads):
+            p = jnp.exp2(s_ref[h, m] - tops[h])
+            s_ref[h, m] = p
+            tot.append(carry[0][h] + fold(p, jnp.sum))
+            acc.append(carry[1][h] + dot(vt_ref[h, m], p.astype(jnp.bfloat16)))
         return tuple(tot), tuple(acc)
 
-    zero_t = tuple(jnp.zeros((dim, blk), jnp.float32) for _ in range(heads))
-    tot, ots = lax.fori_loop(0, pairs + 1, weigh_pair, (tuple(jnp.zeros((8, blk), jnp.float32) for _ in range(heads)), zero_t))
+    zero_t = tuple(jnp.zeros((dim, big), jnp.float32) for _ in range(heads))
+    tot, ots = lax.fori_loop(0, i + 1, weigh_pair, (tuple(jnp.zeros((8, big), jnp.float32) for _ in range(heads)), zero_t))
     inv = [1.0 / jnp.sum(t, axis=0, keepdims=True) for t in tot]
     rs = []
     for h in range(heads):
         o_lo = (ots[h] * inv[h]).astype(jnp.bfloat16)
         rs.append(jnp.sum(dots[h].astype(jnp.float32) * o_lo.astype(jnp.float32), axis=0, keepdims=True))
-        ot_ref[block_of(i), h * dim:(h + 1) * dim, :] = o_lo
-        out_ref[orows, heads * width + h * dim:heads * width + (h + 1) * dim] = o_lo.T
+        ot_ref[i, h * dim:(h + 1) * dim, :] = o_lo
+        out_ref[qrows, heads * width + h * dim:heads * width + (h + 1) * dim] = o_lo.T
 
     def grad_pair(m, acc):
-        new = list(acc)
-        for t in range(2):
-            jx = block_of(2 * m + t)
+        new = []
+        for h in range(heads):
+            v = qkv_ref[rows(m), h * width + 2 * dim:(h + 1) * width]
+            p = s_ref[h, m] * inv[h]
+            ds = (p * (dot(v, dos[h], NT) - rs[h])).astype(jnp.bfloat16)
+            dv_ref[h, m] += dot(p.astype(jnp.bfloat16), dos[h])
+            dk_ref[h, m] += dot(ds, qs[h])
+            new.append(acc[h] + dot(kt_ref[h, m], ds))
+        return tuple(new)
+
+    dqts = lax.fori_loop(0, i + 1, grad_pair, zero_t)
+    for h in range(heads):
+        out_ref[qrows, h * width:h * width + dim] = (dqts[h] * scale).astype(jnp.bfloat16).T
+
+    @pl.when(i == nblk // 2 - 1)
+    def _():
+        for m in range(nblk // 2):
+            at = slice(m * big, (m + 1) * big)
             for h in range(heads):
-                v = qkv_ref[rows(2 * m + t), h * width + 2 * dim:(h + 1) * width]
-                p = s_ref[h, 2 * m + t] * inv[h]
-                ds = (p * (dot(v, dos[h], NT) - rs[h])).astype(jnp.bfloat16)
-                dv_ref[h, jx] += dot(p.astype(jnp.bfloat16), dos[h])
-                dk_ref[h, jx] += dot(ds, qs[h])
-                new[h] = new[h] + dot(kt_ref[h, jx], ds)
-        return tuple(new)
-
-    dqts = lax.fori_loop(0, pairs + 1, grad_pair, zero_t)
-    for h in range(heads):
-        dq = (dqts[h] * scale).astype(jnp.bfloat16).T
-        out_ref[orows, h * width:h * width + dim] = dq
-        dqp_ref[qrows, h * width:h * width + dim] = dq
-
-    @pl.when(i == nblk - 1)
-    def _():
-        for b in range(nblk):
-            r = 2 * (b % (nblk // 2)) + b // (nblk // 2)
-            lrows = pl.ds(pl.multiple_of(jnp.bitwise_xor(me, r) * blk, blk), blk)
-            for h in range(heads):
-                dk = (dk_ref[h, b] * scale).astype(jnp.bfloat16)
-                dv = dv_ref[h, b].astype(jnp.bfloat16)
-                for ref, at in ((out_ref, lrows), (dqp_ref, slice(b * blk, (b + 1) * blk))):
-                    ref[at, h * width + dim:h * width + 2 * dim] = dk
-                    ref[at, h * width + 2 * dim:(h + 1) * width] = dv
+                out_ref[at, h * width + dim:h * width + 2 * dim] = (dk_ref[h, m] * scale).astype(jnp.bfloat16)
+                out_ref[at, h * width + 2 * dim:(h + 1) * width] = dv_ref[h, m].astype(jnp.bfloat16)
 
 
 def stage(me, slopes, x_two, d_two, w, b, wo, pos, gw, gwo, nblk, heads, dim):
     n, hidden = x_two[0].shape
     seq = 2 * n
     blk = seq // nblk
+    half = nblk // 2
     width, owidth = 3 * heads * dim, heads * dim
     tile = hidden // nblk
     first = gw is None
@@ -194,7 +183,7 @@
     tiles = heads * nblk * (nblk + 1) // 2
 
     def late(i):
-        return jnp.maximum(i - 2 * nblk, 0)
+        return jnp.maximum(i - nblk - half, 0)
 
     def fixed(shape):
         return pl.BlockSpec(shape, lambda i, m: (0, 0), pipeline_mode=pl.Buffered(1))
@@ -214,19 +203,18 @@
         body,
         grid_spec=pltpu.PrefetchScalarGridSpec(
             num_scalar_prefetch=1,
-            grid=(3 * nblk,),
+            grid=(2 * nblk + half,),
             in_specs=in_specs,
             out_specs=[pl.BlockSpec((seq, width + owidth), lambda i, m: (0, 0), pipeline_mode=pl.Buffered(1)), gw_spec, gwo_spec],
             scratch_shapes=[
                 pltpu.VMEM((seq, width), jnp.bfloat16),
                 pltpu.VMEM((seq, owidth), jnp.bfloat16),
-                pltpu.VMEM((heads, nblk, blk, blk), jnp.float32),
-                pltpu.VMEM((heads, nblk, blk, dim), jnp.float32),
-                pltpu.VMEM((heads, nblk, blk, dim), jnp.float32),
-                pltpu.VMEM((heads, nblk, dim, blk), jnp.bfloat16),
-                pltpu.VMEM((heads, nblk, dim, blk), jnp.bfloat16),
-                pltpu.VMEM((nblk, owidth, blk), jnp.bfloat16),
-                pltpu.VMEM((seq, width), jnp.bfloat16),
+                pltpu.VMEM((heads, half, 2 * blk, 2 * blk), jnp.float32),
+                pltpu.VMEM((heads, half, 2 * blk, dim), jnp.float32),
+                pltpu.VMEM((heads, half, 2 * blk, dim), jnp.float32),
+                pltpu.VMEM((heads, half, dim, 2 * blk), jnp.bfloat16),
+                pltpu.VMEM((heads, half, dim, 2 * blk), jnp.bfloat16),
+                pltpu.VMEM((half, owidth, 2 * blk), jnp.bfloat16),
                 pltpu.VMEM((nblk, blk, hidden), jnp.bfloat16),
                 pltpu.VMEM((nblk, blk, hidden), jnp.bfloat16),
                 pltpu.SemaphoreType.DMA((nblk,)),
@@ -375,11 +363,21 @@
             d_two = gather_halves(dy_blk[s])
             res, gw, gwo = stage(me_arr, slopes, x_two, d_two, w_mine, b_mine, wo_mine, pos_col[s], gw, gwo,
                                  sp_size, heads, head_dim)
-            parts.append(lax.all_to_all(res.reshape(sp_size, seq_loc, width + owidth), "sp", 0, 0, tiled=True))
+            blocks = res.reshape(sp_size, seq_loc, width + owidth)
+            if s == batch_loc - 2:
+                picks = [lax.dynamic_index_in_dim(blocks, me ^ r, 0) for r in range(sp_size)]
+                parts.append([swap(v, r) if r else v for r, v in enumerate(picks)])
+            else:
+                parts.append(lax.all_to_all(blocks, "sp", 0, 0, tiled=True))
             results.append(res)
         gb_mine = sum(jnp.sum(after(d, gw)[:, :width].astype(jnp.float32), axis=0) for d in results)
 
-        got = jnp.stack(lax.optimization_barrier((parts, gw))[0])
+        got = list(lax.optimization_barrier((parts, gw))[0])
+        joined = jnp.zeros((sp_size, seq_loc, width + owidth), jnp.bfloat16)
+        for r, v in enumerate(got[batch_loc - 2]):
+            joined = lax.dynamic_update_slice(joined, v, (me ^ r, 0, 0))
+        got[batch_loc - 2] = joined
+        got = jnp.stack(got)
         got = jnp.transpose(got, (0, 2, 1, 3))
         dq_loc = got[..., :width].reshape(batch_loc, seq_loc, sp_size * width)
         o_loc = got[..., width:].reshape(batch_loc, seq_loc, hidden)

time: 1310 us -> 1240 us (0.947)
  Pallas kernels: 371 us -> 303 us
  blocking collectives: 104 us -> 52.3 us
  waiting for transfers between devices: 524 us -> 558 us
    pallas_call x4, Pallas kernels: 295 us -> 227 us  [stage(): pl.pallas_call(body, grid_spec=pltpu.PrefetchScalarGridSpec(num_scalar_pr...]
    all_to_all x2 -> x1, blocking collectives: 104 us -> 52.3 us  [block_fn(): parts.append(lax.all_to_all(blocks, 'sp', 0, 0, tiled=True))]
    ppermute x94 -> x101, waiting for transfers between devices: 524 us -> 558 us  [swap(): return lax.ppermute(v, 'sp', [(i, i ^ r) for i in range(sp_size)])]
    ppermute x94 -> x101, starting transfers between devices: 66.4 us -> 71.4 us  [swap(): return lax.ppermute(v, 'sp', [(i, i ^ r) for i in range(sp_size)])]
    unnamed x163 -> x191, local copies, waits for them, and re-layouts: 52.2 us -> 55.8 us
  transfers between devices with their start and end apart: 96 -> 103, of which waited for: 33 -> 37; matrix products, arithmetic and copies ran while one was open for 16% -> 18% of each run, Pallas kernels for 22% -> 19%
where the time goes in v2:
time: 1240 us; the launch traced here: 1230 us
  waiting for transfers between devices  558 us (45%)
  Pallas kernels  303 us (24%)
  local copies, waits for them, and re-layouts  153 us (12%)
  starting transfers between devices  78.4 us (6%)
  blocking collectives  52.3 us (4%)
  matrix products  48.7 us (4%)
  other arithmetic  30.3 us (2%)
    ppermute x101, waiting for transfers between devices, swap(): return lax.ppermute(v, 'sp', [(i, i ^ r) for i in range(sp_size)])  558 us
    pallas_call x4, Pallas kernels, stage(): pl.pallas_call(body, grid_spec=pltpu.PrefetchScalarGridSpec(num_scalar_pr...  227 us
    ppermute x101, starting transfers between devices, swap(): return lax.ppermute(v, 'sp', [(i, i ^ r) for i in range(sp_size)])  71.4 us
    pallas_call x8, Pallas kernels, place(): pl.pallas_call(functools.partial(place_kernel, heads=heads, dim=dim, grou...  62.5 us
    unnamed x191, local copies, waits for them, and re-layouts  55.8 us
    all_to_all x1, blocking collectives, block_fn(): parts.append(lax.all_to_all(blocks, 'sp', 0, 0, tiled=True))  52.3 us
    dot_general x1, matrix products, block_fn(): jnp.einsum('bsk,hk->bsh', dq_loc, w_flat, preferred_element_type=jnp.floa...  36 us
    optimization_barrier x1, local copies, waits for them, and re-layouts, after(): return lax.optimization_barrier((value,) + others)[0]  33.7 us
  transfers between devices with their start and end apart: 103, of which 37 were waited for; matrix products, arithmetic and copies ran while one was open for 18% of the time, Pallas kernels for 19%

profile of v2, /device:TPU:0, one launch (start us, length us, event | category | flops | bytes accessed | tf_op | source)
XLA Modules:
  0.0 1226.2 jit_solution(8708156800487221257)
XLA Ops:
  20.8 33.7 %copy.47 = bf16[2048,16,3,128]{0,3,2,1:T(8,128)(2,1)} copy(bf16[2048,16,3,128]{3,1,2,0:T(8,128)(2,1)} %param.15) | data formatting | bytes 50331648 | tf_op jit(solution)/shard_map/optimization_barrier | solution.py:305
  81.8 11.9 collective-permute-done.42
  98.2 17.8 %collective-permute-done.27 = bf16[256,2048]{1,0:T(8,128)(2,1)S(1)} collective-permute-done((bf16[256,2048]{1,0:T(8,128)(2,1)}, bf16[256,2048]{1,0:T(8,128)(2,1)S(1)}, u32[]{:S(2)}, u32[]{:S(2)}) %collective-permute-start.27) | collective-permute-done | bytes 1048608 | tf_op jit(solution)/shard_map/ppermute | solution.py:312
  120.5 18.1 %collective-permute-done.32 = bf16[256,2048]{1,0:T(8,128)(2,1)} collective-permute-done((bf16[256,2048]{1,0:T(8,128)(2,1)}, bf16[256,2048]{1,0:T(8,128)(2,1)}, u32[]{:S(2)}, u32[]{:S(2)}) %collective-permute-start.32) | collective-permute-done | bytes 1048608 | tf_op jit(solution)/shard_map/ppermute | solution.py:312
  144.9 16.1 %collective-permute-done.17 = bf16[256,2048]{1,0:T(8,128)(2,1)S(1)} collective-permute-done((bf16[256,2048]{1,0:T(8,128)(2,1)}, bf16[256,2048]{1,0:T(8,128)(2,1)S(1)}, u32[]{:S(2)}, u32[]{:S(2)}) %collective-permute-start.17) | collective-permute-done | bytes 1048608 | tf_op jit(solution)/shard_map/ppermute | solution.py:312
  167.5 15.9 %collective-permute-done.22 = bf16[256,2048]{1,0:T(8,128)(2,1)S(1)} collective-permute-done((bf16[256,2048]{1,0:T(8,128)(2,1)S(1)}, bf16[256,2048]{1,0:T(8,128)(2,1)S(1)}, u32[]{:S(2)}, u32[]{:S(2)}) %collective-permute-start.22) | collective-permute-done | bytes 1048608 | tf_op jit(solution)/shard_map/ppermute | solution.py:312
  185.7 10.7 collective-permute-done.39
  208.4 41.8 %collective-permute-done.45 = bf16[128,2048]{1,0:T(8,128)(2,1)S(1)} collective-permute-done((bf16[128,2048]{1,0:T(8,128)(2,1)S(1)}, bf16[128,2048]{1,0:T(8,128)(2,1)S(1)}, u32[]{:S(2)}, u32[]{:S(2)}) %collective-permute-start.45) | collective-permute-done | bytes 524320 | tf_op jit(solution)/shard_map/ppermute | solution.py:312
  343.0 56.3 %stage.4 = (bf16[2048,1024]{1,0:T(8,128)(2,1)}, f32[2048,768]{1,0:T(8,128)}, f32[256,2048]{1,0:T(8,128)}) custom-call(s32[1]{0:T(128)} %bitcast.me_ref, f32[2]{0:T(128)} %exponential_multiply_fusion.slope_ref, bf16[1024,2048]{1,0:T(8,128)(2,1)} %copy-done.57, bf16[1024,2048]{1,0:T(8,128)(2,1)} %copy-done.70, bf16[1024,2048]{1,0:T(8,128)(2,1)} %copy-done.59, ...), custom_call_target="tpu_custom_call" | custom-call | flops 24427626496 | bytes 33554432 | tf_op jit(solution)/shard_map/stage/pallas_call | solution.py:202
  399.8 57.0 %stage.5 = (bf16[2048,1024]{1,0:T(8,128)(2,1)}, f32[2048,768]{1,0:T(8,128)}, f32[256,2048]{1,0:T(8,128)}) custom-call(s32[1]{0:T(128)} %bitcast.me_ref, f32[2]{0:T(128)} %exponential_multiply_fusion.slope_ref, bf16[1024,2048]{1,0:T(8,128)(2,1)} %constant_dynamic-update-slice_fusion.28.x0_ref, ...), custom_call_target="tpu_custom_call", output_to_operand_aliasing={{1}: (10, {}), {2}: (11, {})} | custom-call | flops 24427626496 | bytes 33554432 | tf_op jit(solution)/shard_map/stage/pallas_call | solution.py:202
  456.8 57.2 %stage.6 = (bf16[2048,1024]{1,0:T(8,128)(2,1)}, f32[2048,768]{1,0:T(8,128)}, f32[256,2048]{1,0:T(8,128)}) custom-call(s32[1]{0:T(128)} %bitcast.me_ref, f32[2]{0:T(128)} %exponential_multiply_fusion.slope_ref, bf16[1024,2048]{1,0:T(8,128)(2,1)} %constant_dynamic-update-slice_fusion.18.x0_ref, ...), custom_call_target="tpu_custom_call", output_to_operand_aliasing={{1}: (10, {}), {2}: (11, {})} | custom-call | flops 24427626496 | bytes 33554432 | tf_op jit(solution)/shard_map/stage/pallas_call | solution.py:202
  514.0 57.0 %stage.7 = (bf16[2048,1024]{1,0:T(8,128)(2,1)}, f32[2048,768]{1,0:T(8,128)}, f32[256,2048]{1,0:T(8,128)}) custom-call(s32[1]{0:T(128)} %bitcast.me_ref, f32[2]{0:T(128)} %exponential_multiply_fusion.slope_ref, bf16[1024,2048]{1,0:T(8,128)(2,1)} %constant_dynamic-update-slice_fusion.x0_ref, ...), custom_call_target="tpu_custom_call", output_to_operand_aliasing={{1}: (10, {}), {2}: (11, {})} | custom-call | flops 24427626496 | bytes 33554432 | tf_op jit(solution)/shard_map/stage/pallas_call | solution.py:202
  571.0 52.3 %all_to_all.15 = bf16[8,256,1024]{2,1,0:T(8,128)(2,1)} all-to-all(bf16[8,256,1024]{2,1,0:T(8,128)(2,1)} %bitcast.163), channel_id=1, replica_groups=mesh['dp'=1,'sp'=8] {'sp'}, dimensions={0} | all-to-all | bytes 8388608 | tf_op jit(solution)/shard_map/all_to_all | solution.py:371
  644.9 84.3 %collective-permute-done.48 = bf16[1,256,1024]{2,1,0:T(8,128)(2,1)} collective-permute-done((bf16[1,256,1024]{2,1,0:T(8,128)(2,1)S(1)}, bf16[1,256,1024]{2,1,0:T(8,128)(2,1)}, u32[]{:S(2)}, u32[]{:S(2)}) %collective-permute-start.48) | collective-permute-done | bytes 524320 | tf_op jit(solution)/shard_map/ppermute | solution.py:312
  734.0 45.7 %collective-permute-done.56.p2 = f32[256,768]{1,0:T(8,128)} collective-permute-done((f32[256,768]{1,0:T(8,128)}, f32[256,768]{1,0:T(8,128)}, u32[]{:S(2)}, u32[]{:S(2)}) %collective-permute-start.56) | collective-permute-done | bytes 786464 | tf_op jit(solution)/shard_map/ppermute | solution.py:312
  794.0 99.2 %collective-permute-done.78.p0 = f32[640,768]{1,0:T(8,128)S(1)} collective-permute-done((f32[640,768]{1,0:T(8,128)}, f32[640,768]{1,0:T(8,128)S(1)}, u32[]{:S(2)}, u32[]{:S(2)}) %collective-permute-start.78) | collective-permute-done | bytes 1966112 | tf_op jit(solution)/shard_map/ppermute | solution.py:312
  893.2 18.6 %collective-permute-done.72.p2 = f32[640,768]{1,0:T(8,128)S(1)} collective-permute-done((f32[640,768]{1,0:T(8,128)S(1)}, f32[640,768]{1,0:T(8,128)S(1)}, u32[]{:S(2)}, u32[]{:S(2)}) %collective-permute-start.72) | collective-permute-done | bytes 1966112 | tf_op jit(solution)/shard_map/ppermute | solution.py:312
  913.3 22.0 %collective-permute-done.70.p0 = f32[640,768]{1,0:T(8,128)S(1)} collective-permute-done((f32[640,768]{1,0:T(8,128)S(1)}, f32[640,768]{1,0:T(8,128)S(1)}, u32[]{:S(2)}, u32[]{:S(2)}) %collective-permute-start.70) | collective-permute-done | bytes 1966112 | tf_op jit(solution)/shard_map/ppermute | solution.py:312
  958.5 10.5 collective-permute-done.50
  1026.1 12.4 %collective-permute-done.81 = f32[320,768]{1,0:T(8,128)S(1)} collective-permute-done((f32[320,768]{1,0:T(8,128)S(1)}, f32[320,768]{1,0:T(8,128)S(1)}, u32[]{:S(2)}, u32[]{:S(2)}) %collective-permute-start.81) | collective-permute-done | bytes 983072 | tf_op jit(solution)/shard_map/ppermute | solution.py:312
  1046.1 13.0 %collective-permute-done.73 = f32[320,768]{1,0:T(8,128)S(1)} collective-permute-done((f32[320,768]{1,0:T(8,128)}, f32[320,768]{1,0:T(8,128)S(1)}, u32[]{:S(2)}, u32[]{:S(2)}) %collective-permute-start.73) | collective-permute-done | bytes 983072 | tf_op jit(solution)/shard_map/ppermute | solution.py:312
  1067.3 36.0 %fusion.10 = (f32[2048]{0:T(1024)S(1)}, f32[4,256]{1,0:T(4,128)}, f32[4,256]{1,0:T(4,128)}, f32[2048]{0:T(1024)S(1)}, f32[4,256,2048]{2,1,0:T(8,128)S(1)}) fusion(bf16[4,256,2048]{2,1,0:T(8,128)(2,1)S(1)} %copy-done.2, f32[4,256]{1,0:T(4,128)} %add_rsqrt_fusion, f32[4,256]{1,0:T(4,128)S(1)} %broadcast_multiply_fusion.2, f32[2048]{0:T(1024)} %param.13, ...), kind=kOutput, calls=%fused_computation.17 | convolution fusion | flops 25790769152 | bytes 50372608 | tf_op jit(solution)/shard_map/bsk,hk->bsh/dot_general | solution.py:386
  1129.4 12.7 %fusion.13 = bf16[4,256,2048]{2,1,0:T(8,128)(2,1)} fusion(bf16[4,256,2048]{2,1,0:T(8,128)(2,1)S(1)} %copy-done.2, f32[2048]{0:T(1024)S(1)} %copy-done.72, bf16[4,256,2048]{2,1,0:T(8,128)(2,1)S(1)} %bitcast.166, bf16[2048,2048]{1,0:T(8,128)(2,1)} %param.17), kind=kOutput, calls=%fused_computation.20 | convolution fusion | flops 8598323200 | bytes 20979712 | tf_op jit(solution)/shard_map/bsh,hk->bsk/dot_general | solution.py:385
  1212.5 13.5 %stack_rows.1 = f32[8,256,2048]{2,1,0:T(8,128)} custom-call(s32[1]{0:T(128)} %bitcast.me_ref, f32[256,2048]{1,0:T(8,128)} %get-tuple-element.67.refs_0_, f32[256,2048]{1,0:T(8,128)} %collective-permute-done.93.refs_1_, f32[256,2048]{1,0:T(8,128)} %collective-permute-done.94.refs_2_, f32[256,2048]{1,0:T(8,128)} %collective-permute-done.95.refs_3_, ...), custom_call_target="tpu_custom_call" | custom-call | flops 16777216 | bytes 33554432 | tf_op jit(solution)/shard_map/stack_rows/pallas_call | solution.py:287
  (497 shorter events, 410.2 us)
Async XLA Ops:
  253.3 85.8 %collective-permute-start.41 = (bf16[1024,2048]{1,0:T(8,128)(2,1)S(1)}, bf16[1024,2048]{1,0:T(8,128)(2,1)S(1)}, u32[]{:S(2)}, u32[]{:S(2)}) collective-permute-start(bf16[1024,2048]{1,0:T(8,128)(2,1)S(1)} %constant_dynamic-update-slice_fusion.38.x0_ref), channel_id=1, source_target_pairs={{0,1},{1,0},{2,3},{3,2},{4,5},{5,4},{6,7},{7,6}} | collective-permute-start | bytes 12582920 | tf_op jit(solution)/shard_map/ppermute | solution.py:312
  253.3 86.3 %collective-permute-start.46 = (bf16[1024,2048]{1,0:T(8,128)(2,1)S(1)}, bf16[1024,2048]{1,0:T(8,128)(2,1)S(1)}, u32[]{:S(2)}, u32[]{:S(2)}) collective-permute-start(bf16[1024,2048]{1,0:T(8,128)(2,1)S(1)} %constant_dynamic-update-slice_fusion.43.d0_ref), channel_id=1, source_target_pairs={{0,1},{1,0},{2,3},{3,2},{4,5},{5,4},{6,7},{7,6}} | collective-permute-start | bytes 12582920 | tf_op jit(solution)/shard_map/ppermute | solution.py:312
  300.6 98.8 %collective-permute-start.31 = (bf16[1024,2048]{1,0:T(8,128)(2,1)}, bf16[1024,2048]{1,0:T(8,128)(2,1)}, u32[]{:S(2)}, u32[]{:S(2)}) collective-permute-start(bf16[1024,2048]{1,0:T(8,128)(2,1)} %constant_dynamic-update-slice_fusion.28.x0_ref), channel_id=1, source_target_pairs={{0,1},{1,0},{2,3},{3,2},{4,5},{5,4},{6,7},{7,6}} | collective-permute-start | bytes 12582920 | tf_op jit(solution)/shard_map/ppermute | solution.py:312
  308.4 91.4 %collective-permute-start.36 = (bf16[1024,2048]{1,0:T(8,128)(2,1)}, bf16[1024,2048]{1,0:T(8,128)(2,1)}, u32[]{:S(2)}, u32[]{:S(2)}) collective-permute-start(bf16[1024,2048]{1,0:T(8,128)(2,1)} %constant_dynamic-update-slice_fusion.33.d0_ref), channel_id=1, source_target_pairs={{0,1},{1,0},{2,3},{3,2},{4,5},{5,4},{6,7},{7,6}} | collective-permute-start | bytes 12582920 | tf_op jit(solution)/shard_map/ppermute | solution.py:312
  338.2 118.6 %collective-permute-start.21 = (bf16[1024,2048]{1,0:T(8,128)(2,1)}, bf16[1024,2048]{1,0:T(8,128)(2,1)}, u32[]{:S(2)}, u32[]{:S(2)}) collective-permute-start(bf16[1024,2048]{1,0:T(8,128)(2,1)} %constant_dynamic-update-slice_fusion.18.x0_ref), channel_id=1, source_target_pairs={{0,1},{1,0},{2,3},{3,2},{4,5},{5,4},{6,7},{7,6}} | collective-permute-start | bytes 12582920 | tf_op jit(solution)/shard_map/ppermute | solution.py:312
  339.1 117.7 %collective-permute-start.26 = (bf16[1024,2048]{1,0:T(8,128)(2,1)}, bf16[1024,2048]{1,0:T(8,128)(2,1)}, u32[]{:S(2)}, u32[]{:S(2)}) collective-permute-start(bf16[1024,2048]{1,0:T(8,128)(2,1)} %constant_dynamic-update-slice_fusion.23.d0_ref), channel_id=1, source_target_pairs={{0,1},{1,0},{2,3},{3,2},{4,5},{5,4},{6,7},{7,6}} | collective-permute-start | bytes 12582920 | tf_op jit(solution)/shard_map/ppermute | solution.py:312
  341.0 173.0 %collective-permute-start.4 = (bf16[1024,2048]{1,0:T(8,128)(2,1)}, bf16[1024,2048]{1,0:T(8,128)(2,1)}, u32[]{:S(2)}, u32[]{:S(2)}) collective-permute-start(bf16[1024,2048]{1,0:T(8,128)(2,1)} %constant_dynamic-update-slice_fusion.x0_ref), channel_id=1, source_target_pairs={{0,1},{1,0},{2,3},{3,2},{4,5},{5,4},{6,7},{7,6}} | collective-permute-start | bytes 12582920 | tf_op jit(solution)/shard_map/ppermute | solution.py:312
  399.3 114.7 %collective-permute-start.9 = (bf16[1024,2048]{1,0:T(8,128)(2,1)}, bf16[1024,2048]{1,0:T(8,128)(2,1)}, u32[]{:S(2)}, u32[]{:S(2)}) collective-permute-start(bf16[1024,2048]{1,0:T(8,128)(2,1)} %constant_dynamic-update-slice_fusion.5.d0_ref), channel_id=1, source_target_pairs={{0,1},{1,0},{2,3},{3,2},{4,5},{5,4},{6,7},{7,6}} | collective-permute-start | bytes 12582920 | tf_op jit(solution)/shard_map/ppermute | solution.py:312
  623.4 107.3 %all-to-all-start.1 = ((bf16[8,256,1024]{2,1,0:T(8,128)(2,1)}), bf16[8,256,1024]{2,1,0:T(8,128)(2,1)}, u32[]{:S(2)}, u32[]{:S(2)}) async-start(bf16[8,256,1024]{2,1,0:T(8,128)(2,1)} %bitcast.162), calls=%async_computation.1 | async-start | bytes 8388608 | tf_op jit(solution)/shard_map/all_to_all | solution.py:371
  630.8 155.9 %collective-permute-start.80 = (f32[640,768]{1,0:T(8,128)}, f32[640,768]{1,0:T(8,128)}, u32[]{:S(2)}, u32[]{:S(2)}) collective-permute-start(f32[640,768]{1,0:T(8,128)} %get-tuple-element.112.p0), channel_id=1, source_target_pairs={{0,2},{1,3},{2,0},{3,1},{4,6},{5,7},{6,4},{7,5}} | collective-permute-start | bytes 5898248 | tf_op jit(solution)/shard_map/ppermute | solution.py:312
  636.9 92.3 %collective-permute-start.48 = (bf16[1,256,1024]{2,1,0:T(8,128)(2,1)S(1)}, bf16[1,256,1024]{2,1,0:T(8,128)(2,1)}, u32[]{:S(2)}, u32[]{:S(2)}) collective-permute-start(bf16[1,256,1024]{2,1,0:T(8,128)(2,1)S(1)} %get-tuple-element.125), channel_id=1, source_target_pairs={{0,2},{1,3},{2,0},{3,1},{4,6},{5,7},{6,4},{7,5}} | collective-permute-start | bytes 1572872 | tf_op jit(solution)/shard_map/ppermute | solution.py:312
  639.3 145.4 %collective-permute-start.64 = (f32[512,768]{1,0:T(8,128)S(1)}, f32[512,768]{1,0:T(8,128)}, u32[]{:S(2)}, u32[]{:S(2)}) collective-permute-start(f32[512,768]{1,0:T(8,128)S(1)} %slice.202.p0), channel_id=1, source_target_pairs={{0,2},{1,3},{2,0},{3,1},{4,6},{5,7},{6,4},{7,5}} | collective-permute-start | bytes 4718600 | tf_op jit(solution)/shard_map/ppermute | solution.py:312
  640.5 144.2 %collective-permute-start.62 = (f32[512,768]{1,0:T(8,128)S(1)}, f32[512,768]{1,0:T(8,128)}, u32[]{:S(2)}, u32[]{:S(2)}) collective-permute-start(f32[512,768]{1,0:T(8,128)S(1)} %slice.202.p0), channel_id=1, source_target_pairs={{0,4},{1,5},{2,6},{3,7},{4,0},{5,1},{6,2},{7,3}} | collective-permute-start | bytes 4718600 | tf_op jit(solution)/shard_map/ppermute | solution.py:312
  644.1 135.7 %collective-permute-start.56 = (f32[256,768]{1,0:T(8,128)}, f32[256,768]{1,0:T(8,128)}, u32[]{:S(2)}, u32[]{:S(2)}) collective-permute-start(f32[256,768]{1,0:T(8,128)} %slice.199.p0), channel_id=1, source_target_pairs={{0,2},{1,3},{2,0},{3,1},{4,6},{5,7},{6,4},{7,5}} | collective-permute-start | bytes 2359304 | tf_op jit(solution)/shard_map/ppermute | solution.py:312
  730.7 250.8 %all-to-all-start = ((bf16[8,256,1024]{2,1,0:T(8,128)(2,1)}), bf16[8,256,1024]{2,1,0:T(8,128)(2,1)}, u32[]{:S(2)}, u32[]{:S(2)}) async-start(bf16[8,256,1024]{2,1,0:T(8,128)(2,1)} %bitcast.161), calls=%async_computation | async-start | bytes 8388608 | tf_op jit(solution)/shard_map/all_to_all | solution.py:371
  779.8 155.5 %collective-permute-start.94 = (f32[256,2048]{1,0:T(8,128)}, f32[256,2048]{1,0:T(8,128)}, u32[]{:S(2)}, u32[]{:S(2)}) collective-permute-start(f32[256,2048]{1,0:T(8,128)} %get-tuple-element.67.refs_0_), channel_id=1, source_target_pairs={{0,2},{1,3},{2,0},{3,1},{4,6},{5,7},{6,4},{7,5}} | collective-permute-start | bytes 6291464 | tf_op jit(solution)/shard_map/ppermute | solution.py:312
  779.8 155.5 %collective-permute-start.96 = (f32[256,2048]{1,0:T(8,128)}, f32[256,2048]{1,0:T(8,128)}, u32[]{:S(2)}, u32[]{:S(2)}) collective-permute-start(f32[256,2048]{1,0:T(8,128)} %get-tuple-element.67.refs_0_), channel_id=1, source_target_pairs={{0,4},{1,5},{2,6},{3,7},{4,0},{5,1},{6,2},{7,3}} | collective-permute-start | bytes 6291464 | tf_op jit(solution)/shard_map/ppermute | solution.py:312
  784.6 108.5 %collective-permute-start.78 = (f32[640,768]{1,0:T(8,128)}, f32[640,768]{1,0:T(8,128)S(1)}, u32[]{:S(2)}, u32[]{:S(2)}) collective-permute-start(f32[640,768]{1,0:T(8,128)} %get-tuple-element.112.p0), channel_id=1, source_target_pairs={{0,4},{1,5},{2,6},{3,7},{4,0},{5,1},{6,2},{7,3}} | collective-permute-start | bytes 5898248 | tf_op jit(solution)/shard_map/ppermute | solution.py:312
  784.7 127.0 %collective-permute-start.72 = (f32[640,768]{1,0:T(8,128)S(1)}, f32[640,768]{1,0:T(8,128)S(1)}, u32[]{:S(2)}, u32[]{:S(2)}) collective-permute-start(f32[640,768]{1,0:T(8,128)S(1)} %get-tuple-element.113.p0), channel_id=1, source_target_pairs={{0,2},{1,3},{2,0},{3,1},{4,6},{5,7},{6,4},{7,5}} | collective-permute-start | bytes 5898248 | tf_op jit(solution)/shard_map/ppermute | solution.py:312
  786.7 148.6 %collective-permute-start.70 = (f32[640,768]{1,0:T(8,128)S(1)}, f32[640,768]{1,0:T(8,128)S(1)}, u32[]{:S(2)}, u32[]{:S(2)}) collective-permute-start(f32[640,768]{1,0:T(8,128)S(1)} %get-tuple-element.113.p0), channel_id=1, source_target_pairs={{0,4},{1,5},{2,6},{3,7},{4,0},{5,1},{6,2},{7,3}} | collective-permute-start | bytes 5898248 | tf_op jit(solution)/shard_map/ppermute | solution.py:312
  1128.0 84.5 %collective-permute-start.93 = (f32[256,2048]{1,0:T(8,128)}, f32[256,2048]{1,0:T(8,128)}, u32[]{:S(2)}, u32[]{:S(2)}) collective-permute-start(f32[256,2048]{1,0:T(8,128)} %get-tuple-element.67.refs_0_), channel_id=1, source_target_pairs={{0,1},{1,0},{2,3},{3,2},{4,5},{5,4},{6,7},{7,6}} | collective-permute-start | bytes 6291464 | tf_op jit(solution)/shard_map/ppermute | solution.py:312
  1128.3 84.1 %collective-permute-start.95 = (f32[256,2048]{1,0:T(8,128)}, f32[256,2048]{1,0:T(8,128)}, u32[]{:S(2)}, u32[]{:S(2)}) collective-permute-start(f32[256,2048]{1,0:T(8,128)} %collective-permute-done.94.refs_2_), channel_id=1, source_target_pairs={{0,1},{1,0},{2,3},{3,2},{4,5},{5,4},{6,7},{7,6}} | collective-permute-start | bytes 6291464 | tf_op jit(solution)/shard_map/ppermute | solution.py:312
  1128.5 83.9 %collective-permute-start.97 = (f32[256,2048]{1,0:T(8,128)}, f32[256,2048]{1,0:T(8,128)}, u32[]{:S(2)}, u32[]{:S(2)}) collective-permute-start(f32[256,2048]{1,0:T(8,128)} %collective-permute-done.96.refs_4_), channel_id=1, source_target_pairs={{0,1},{1,0},{2,3},{3,2},{4,5},{5,4},{6,7},{7,6}} | collective-permute-start | bytes 6291464 | tf_op jit(solution)/shard_map/ppermute | solution.py:312
  1129.1 83.4 %collective-permute-start.100 = (f32[256,2048]{1,0:T(8,128)}, f32[256,2048]{1,0:T(8,128)}, u32[]{:S(2)}, u32[]{:S(2)}) collective-permute-start(f32[256,2048]{1,0:T(8,128)} %constant_dynamic-update-slice_fusion.56.refs_6_), channel_id=1, source_target_pairs={{0,1},{1,0},{2,3},{3,2},{4,5},{5,4},{6,7},{7,6}} | collective-permute-start | bytes 6291464 | tf_op jit(solution)/shard_map/ppermute | solution.py:312
  (152 other events, 4494.0 us)

commit v3 on v2

--- a/solution.py
+++ b/solution.py
@@ -21,7 +21,9 @@
     return lax.dot_general(a, b, dims, preferred_element_type=jnp.float32)
 
 
-def stage_kernel(me_ref, slope_ref, x0_ref, x1_ref, d0_ref, d1_ref, w_ref, b_ref, wo_ref, pos_ref, *refs, nblk, blk, dim, heads, scale, first):
+def stage_kernel(me_ref, slope_ref, w_ref, b_ref, wo_ref, pos_ref, *refs, nblk, blk, dim, heads, scale, first):
+    count = nblk + 2
+    x_pieces, d_pieces, refs = refs[:count], refs[count:2 * count], refs[2 * count:]
     if first:
         gwi_ref = gwoi_ref = None
     else:
@@ -34,9 +36,17 @@
     half = nblk // 2
 
     def load(b):
-        p, at = b // half, pl.ds((b % half) * blk, blk)
-        return (pltpu.make_async_copy((x0_ref, x1_ref)[p].at[at], xv_ref.at[b], x_sem.at[b]),
-                pltpu.make_async_copy((d0_ref, d1_ref)[p].at[at], dv_all_ref.at[b], d_sem.at[b]))
+        p, q = b // half, b % half
+        copies = []
+        for pieces, dst, sem in ((x_pieces, xv_ref, x_sem), (d_pieces, dv_all_ref, d_sem)):
+            base = p * (half + 1)
+            if q < half - 1:
+                copies.append(pltpu.make_async_copy(pieces[base + q], dst.at[b], sem.at[b]))
+            else:
+                for e in range(2):
+                    at = pl.ds(e * (blk // 2), blk // 2)
+                    copies.append(pltpu.make_async_copy(pieces[base + q + e], dst.at[b, at], sem.at[b if e == 0 else nblk + p]))
+        return copies
 
     @pl.when(step == 0)
     def _():
@@ -172,9 +182,8 @@
 
 
 def stage(me, slopes, x_two, d_two, w, b, wo, pos, gw, gwo, nblk, heads, dim):
-    n, hidden = x_two[0].shape
-    seq = 2 * n
-    blk = seq // nblk
+    blk, hidden = x_two[0].shape
+    seq = nblk * blk
     half = nblk // 2
     width, owidth = 3 * heads * dim, heads * dim
     tile = hidden // nblk
@@ -190,14 +199,14 @@
 
     gw_spec = pl.BlockSpec((tile, width), lambda i, m: (late(i), 0))
     gwo_spec = pl.BlockSpec((owidth, tile), lambda i, m: (0, late(i)))
-    args = [x_two[0], x_two[1], d_two[0], d_two[1], w, b, wo, pos]
-    in_specs = [pl.BlockSpec(memory_space=pltpu.SMEM)] + [pl.BlockSpec(memory_space=pl.ANY)] * 4 + [
-                fixed(w.shape), fixed(b.shape), fixed(wo.shape), fixed(pos.shape)]
+    args = [w, b, wo, pos, *x_two, *d_two]
+    in_specs = [pl.BlockSpec(memory_space=pltpu.SMEM), fixed(w.shape), fixed(b.shape), fixed(wo.shape), fixed(pos.shape)]
+    in_specs += [pl.BlockSpec(memory_space=pl.ANY)] * (2 * (nblk + 2))
     aliases = {}
     if not first:
+        aliases = {len(args) + 2: 1, len(args) + 3: 2}
         args += [gw, gwo]
         in_specs += [gw_spec, gwo_spec]
-        aliases = {10: 1, 11: 2}
     flops = tiles * 12 * blk * blk * dim + 4 * seq * hidden * (width + owidth)
     return pl.pallas_call(
         body,
@@ -217,8 +226,8 @@
                 pltpu.VMEM((half, owidth, 2 * blk), jnp.bfloat16),
                 pltpu.VMEM((nblk, blk, hidden), jnp.bfloat16),
                 pltpu.VMEM((nblk, blk, hidden), jnp.bfloat16),
-                pltpu.SemaphoreType.DMA((nblk,)),
-                pltpu.SemaphoreType.DMA((nblk,)),
+                pltpu.SemaphoreType.DMA((nblk + 2,)),
+                pltpu.SemaphoreType.DMA((nblk + 2,)),
             ],
         ),
         out_shape=[jax.ShapeDtypeStruct((seq, width + owidth), jnp.bfloat16),
@@ -298,7 +307,7 @@
     )(me, *pieces)
 
 
-CHUNKS = (640, 640, 512, 256)
+CHUNKS = (768, 640, 384, 256)
 
 
 def after(value, *others):
@@ -317,11 +326,11 @@
         bd = jnp.concatenate([swap(bx[:half], 4), swap(by[half:], 2)], 0)
         return [b, bs, bx, swap(bx, 1), by, swap(by, 1), bd, swap(bd, 1)]
 
-    def gather_halves(b):
+    def gather_pieces(b):
         half = b.shape[0] // 2
-        bx, by = swap(b, 2), swap(b, 4)
-        mine = jnp.concatenate([b, bx, by, swap(bx[:half], 4), swap(by[half:], 2)], 0)
-        return mine, swap(mine, 1)
+        bx, by, bs = swap(b, 2), swap(b, 4), swap(b, 1)
+        d1, d2 = swap(bx[:half], 4), swap(by[half:], 2)
+        return [b, bx, by, d1, d2, bs, swap(bx, 1), swap(by, 1), swap(d1, 1), swap(d2, 1)]
 
     def block_fn(x_blk, pos_blk, keep_blk, ln_gain, ln_bias, w_qkv, b_qkv, w_out, b_out, dy_blk):
         batch_loc, seq_loc, hidden = x_blk.shape
@@ -359,8 +368,8 @@
         gw = gwo = None
         results, parts = [], []
         for s in range(batch_loc):
-            x_two = gather_halves(x_norms[s])
-            d_two = gather_halves(dy_blk[s])
+            x_two = gather_pieces(x_norms[s])
+            d_two = gather_pieces(dy_blk[s])
             res, gw, gwo = stage(me_arr, slopes, x_two, d_two, w_mine, b_mine, wo_mine, pos_col[s], gw, gwo,
                                  sp_size, heads, head_dim)
             blocks = res.reshape(sp_size, seq_loc, width + owidth)
@@ -402,8 +411,11 @@
         grad_w_qkv = None
         group = sp_size // 2
         row = 0
-        for n in CHUNKS:
+        for g, n in enumerate(CHUNKS):
             pieces = gather(gw[row:row + n])
+            if g == 1:
+                pieces[0], grad_b_qkv, grad_gain, grad_bias, grad_b_out = lax.optimization_barrier(
+                    (pieces[0], grad_b_qkv, grad_gain, grad_bias, grad_b_out))
             for far in (0, 1):
                 grad_w_qkv = place(me_arr, pieces[far * group:(far + 1) * group], far, row, grad_w_qkv,
                                    (hidden, 3, num_heads, head_dim), heads, head_dim)

time: 1240 us -> 1190 us (0.960)
  blocking collectives: 52.3 us -> 0 us
  starting transfers between devices: 78.4 us -> 122 us
  local copies, waits for them, and re-layouts: 153 us -> 122 us
    all_to_all x1 -> x0, blocking collectives: 52.3 us -> none  [block_fn(): parts.append(lax.all_to_all(blocks, 'sp', 0, 0, tiled=True))]
    ppermute x101 -> x133, starting transfers between devices: 71.4 us -> 112 us  [swap(): return lax.ppermute(v, 'sp', [(i, i ^ r) for i in range(sp_size)])]
    unnamed x191 -> x242, local copies, waits for them, and re-layouts: 55.8 us -> 23.6 us
    ppermute x101 -> x133, waiting for transfers between devices: 558 us -> 551 us  [swap(): return lax.ppermute(v, 'sp', [(i, i ^ r) for i in range(sp_size)])]
  transfers between devices with their start and end apart: 103 -> 136, of which waited for: 37 -> 44; matrix products, arithmetic and copies ran while one was open for 18% -> 16% of each run, Pallas kernels for 19% -> 26%
where the time goes in v3:
time: 1190 us; the launch traced here: 1180 us
  waiting for transfers between devices  551 us (46%)
  Pallas kernels  305 us (26%)
  local copies, waits for them, and re-layouts  122 us (10%)
  starting transfers between devices  122 us (10%)
  matrix products  49.3 us (4%)
  other arithmetic  25.6 us (2%)
    ppermute x133, waiting for transfers between devices, swap(): return lax.ppermute(v, 'sp', [(i, i ^ r) for i in range(sp_size)])  551 us
    pallas_call x4, Pallas kernels, stage(): pl.pallas_call(body, grid_spec=pltpu.PrefetchScalarGridSpec(num_scalar_pr...  229 us
    ppermute x133, starting transfers between devices, swap(): return lax.ppermute(v, 'sp', [(i, i ^ r) for i in range(sp_size)])  112 us
    pallas_call x8, Pallas kernels, place(): pl.pallas_call(functools.partial(place_kernel, heads=heads, dim=dim, grou...  62.7 us
    dot_general x1, matrix products, block_fn(): jnp.einsum('bsk,hk->bsh', dq_loc, w_flat, preferred_element_type=jnp.floa...  35.4 us
    optimization_barrier x1, local copies, waits for them, and re-layouts, after(): return lax.optimization_barrier((value,) + others)[0]  33.7 us
  transfers between devices with their start and end apart: 136, of which 44 were waited for; matrix products, arithmetic and copies ran while one was open for 16% of the time, Pallas kernels for 26%

profile of v3, /device:TPU:0, one launch (start us, length us, event | category | flops | bytes accessed | tf_op | source)
XLA Modules:
  0.0 1177.0 jit_solution(5410563299629037050)
XLA Ops:
  16.2 40.4 %collective-permute-done.1 = s32[2,4,256]{2,1,0:T(4,128)S(1)} collective-permute-done((s32[2,4,256]{2,1,0:T(4,128)S(1)}, s32[2,4,256]{2,1,0:T(4,128)S(1)}, u32[]{:S(2)}, u32[]{:S(2)}) %collective-permute-start.1) | collective-permute-done | bytes 8224 | tf_op jit(solution)/shard_map/ppermute | solution.py:321
  78.8 22.2 %collective-permute-done.17.refs_12_ = bf16[256,2048]{1,0:T(8,128)(2,1)S(1)} collective-permute-done((bf16[256,2048]{1,0:T(8,128)(2,1)S(1)}, bf16[256,2048]{1,0:T(8,128)(2,1)S(1)}, u32[]{:S(2)}, u32[]{:S(2)}) %collective-permute-start.17) | collective-permute-done | bytes 1048608 | tf_op jit(solution)/shard_map/ppermute | solution.py:321
  104.3 19.2 %collective-permute-done.26.refs_2_ = bf16[256,2048]{1,0:T(8,128)(2,1)S(1)} collective-permute-done((bf16[256,2048]{1,0:T(8,128)(2,1)S(1)}, bf16[256,2048]{1,0:T(8,128)(2,1)S(1)}, u32[]{:S(2)}, u32[]{:S(2)}) %collective-permute-start.26) | collective-permute-done | bytes 1048608 | tf_op jit(solution)/shard_map/ppermute | solution.py:321
  126.8 19.3 %collective-permute-done.35.refs_12_ = bf16[256,2048]{1,0:T(8,128)(2,1)} collective-permute-done((bf16[256,2048]{1,0:T(8,128)(2,1)S(1)}, bf16[256,2048]{1,0:T(8,128)(2,1)}, u32[]{:S(2)}, u32[]{:S(2)}) %collective-permute-start.35) | collective-permute-done | bytes 1048608 | tf_op jit(solution)/shard_map/ppermute | solution.py:321
  149.3 19.1 %collective-permute-done.44.refs_2_ = bf16[256,2048]{1,0:T(8,128)(2,1)S(1)} collective-permute-done((bf16[256,2048]{1,0:T(8,128)(2,1)S(1)}, bf16[256,2048]{1,0:T(8,128)(2,1)S(1)}, u32[]{:S(2)}, u32[]{:S(2)}) %collective-permute-start.44) | collective-permute-done | bytes 1048608 | tf_op jit(solution)/shard_map/ppermute | solution.py:321
  171.7 19.2 %collective-permute-done.53.refs_12_ = bf16[256,2048]{1,0:T(8,128)(2,1)S(1)} collective-permute-done((bf16[256,2048]{1,0:T(8,128)(2,1)S(1)}, bf16[256,2048]{1,0:T(8,128)(2,1)S(1)}, u32[]{:S(2)}, u32[]{:S(2)}) %collective-permute-start.53) | collective-permute-done | bytes 1048608 | tf_op jit(solution)/shard_map/ppermute | solution.py:321
  196.3 17.0 %collective-permute-done.62.refs_2_ = bf16[256,2048]{1,0:T(8,128)(2,1)S(1)} collective-permute-done((bf16[256,2048]{1,0:T(8,128)(2,1)S(1)}, bf16[256,2048]{1,0:T(8,128)(2,1)S(1)}, u32[]{:S(2)}, u32[]{:S(2)}) %collective-permute-start.62) | collective-permute-done | bytes 1048608 | tf_op jit(solution)/shard_map/ppermute | solution.py:321
  217.3 18.6 %collective-permute-done.71.refs_12_ = bf16[256,2048]{1,0:T(8,128)(2,1)S(1)} collective-permute-done((bf16[256,2048]{1,0:T(8,128)(2,1)S(1)}, bf16[256,2048]{1,0:T(8,128)(2,1)S(1)}, u32[]{:S(2)}, u32[]{:S(2)}) %collective-permute-start.71) | collective-permute-done | bytes 1048608 | tf_op jit(solution)/shard_map/ppermute | solution.py:321
  260.2 33.7 %copy.47 = bf16[2048,16,3,128]{0,3,2,1:T(8,128)(2,1)} copy(bf16[2048,16,3,128]{3,1,2,0:T(8,128)(2,1)} %param.15) | data formatting | bytes 50331648 | tf_op jit(solution)/shard_map/optimization_barrier | solution.py:314
  354.1 56.8 %stage.4 = (bf16[2048,1024]{1,0:T(8,128)(2,1)}, f32[2048,768]{1,0:T(8,128)}, f32[256,2048]{1,0:T(8,128)}) custom-call(s32[1]{0:T(128)} %bitcast.me_ref, f32[2]{0:T(128)} %exponential_multiply_fusion.slope_ref, bf16[2048,768]{1,0:T(8,128)(2,1)} %copy.60.w_ref, f32[1,768]{1,0:T(1,128)} %constant_dynamic-slice_fusion.9.b_ref, ...), custom_call_target="tpu_custom_call" | custom-call | flops 24427626496 | bytes 33554432 | tf_op jit(solution)/shard_map/stage/pallas_call | solution.py:211
  426.2 57.4 %stage.5 = (bf16[2048,1024]{1,0:T(8,128)(2,1)}, f32[2048,768]{1,0:T(8,128)}, f32[256,2048]{1,0:T(8,128)}) custom-call(s32[1]{0:T(128)} %bitcast.me_ref, f32[2]{0:T(128)} %exponential_multiply_fusion.slope_ref, bf16[2048,768]{1,0:T(8,128)(2,1)} %copy.60.w_ref, ...), custom_call_target="tpu_custom_call", output_to_operand_aliasing={{1}: (26, {}), {2}: (27, {})} | custom-call | flops 24427626496 | bytes 33554432 | tf_op jit(solution)/shard_map/stage/pallas_call | solution.py:211
  488.8 57.3 %stage.6 = (bf16[2048,1024]{1,0:T(8,128)(2,1)}, f32[2048,768]{1,0:T(8,128)}, f32[256,2048]{1,0:T(8,128)}) custom-call(s32[1]{0:T(128)} %bitcast.me_ref, f32[2]{0:T(128)} %exponential_multiply_fusion.slope_ref, bf16[2048,768]{1,0:T(8,128)(2,1)} %copy.60.w_ref, ...), custom_call_target="tpu_custom_call", output_to_operand_aliasing={{1}: (26, {}), {2}: (27, {})} | custom-call | flops 24427626496 | bytes 33554432 | tf_op jit(solution)/shard_map/stage/pallas_call | solution.py:211
  546.2 57.7 %stage.7 = (bf16[2048,1024]{1,0:T(8,128)(2,1)}, f32[2048,768]{1,0:T(8,128)}, f32[256,2048]{1,0:T(8,128)}) custom-call(s32[1]{0:T(128)} %bitcast.me_ref, f32[2]{0:T(128)} %exponential_multiply_fusion.slope_ref, bf16[2048,768]{1,0:T(8,128)(2,1)} %copy.60.w_ref, ...), custom_call_target="tpu_custom_call", output_to_operand_aliasing={{1}: (26, {}), {2}: (27, {})} | custom-call | flops 24427626496 | bytes 33554432 | tf_op jit(solution)/shard_map/stage/pallas_call | solution.py:211
  620.4 49.3 %collective-permute-done.86.p0 = f32[256,768]{1,0:T(8,128)} collective-permute-done((f32[256,768]{1,0:T(8,128)}, f32[256,768]{1,0:T(8,128)}, u32[]{:S(2)}, u32[]{:S(2)}) %collective-permute-start.86) | collective-permute-done | bytes 786464 | tf_op jit(solution)/shard_map/ppermute | solution.py:321
  677.4 17.6 %collective-permute-done.94.p0 = f32[384,768]{1,0:T(8,128)} collective-permute-done((f32[384,768]{1,0:T(8,128)S(1)}, f32[384,768]{1,0:T(8,128)}, u32[]{:S(2)}, u32[]{:S(2)}) %collective-permute-start.94) | collective-permute-done | bytes 1179680 | tf_op jit(solution)/shard_map/ppermute | solution.py:321
  717.3 30.9 %collective-permute-done.89 = f32[128,768]{1,0:T(8,128)S(1)} collective-permute-done((f32[128,768]{1,0:T(8,128)S(1)}, f32[128,768]{1,0:T(8,128)S(1)}, u32[]{:S(2)}, u32[]{:S(2)}) %collective-permute-start.89) | collective-permute-done | bytes 393248 | tf_op jit(solution)/shard_map/ppermute | solution.py:321
  769.7 76.9 %collective-permute-done.104.p2 = f32[640,768]{1,0:T(8,128)} collective-permute-done((f32[640,768]{1,0:T(8,128)}, f32[640,768]{1,0:T(8,128)}, u32[]{:S(2)}, u32[]{:S(2)}) %collective-permute-start.104) | collective-permute-done | bytes 1966112 | tf_op jit(solution)/shard_map/ppermute | solution.py:321
  846.6 44.9 %collective-permute-done.126.refs_2_ = f32[256,2048]{1,0:T(8,128)} collective-permute-done((f32[256,2048]{1,0:T(8,128)}, f32[256,2048]{1,0:T(8,128)}, u32[]{:S(2)}, u32[]{:S(2)}) %collective-permute-start.126) | collective-permute-done | bytes 2097184 | tf_op jit(solution)/shard_map/ppermute | solution.py:321
  911.1 17.6 %collective-permute-done.82 = bf16[1,256,1024]{2,1,0:T(8,128)(2,1)S(1)} collective-permute-done((bf16[1,256,1024]{2,1,0:T(8,128)(2,1)S(1)}, bf16[1,256,1024]{2,1,0:T(8,128)(2,1)S(1)}, u32[]{:S(2)}, u32[]{:S(2)}) %collective-permute-start.82) | collective-permute-done | bytes 524320 | tf_op jit(solution)/shard_map/ppermute | solution.py:321
  961.9 28.2 %collective-permute-done.105 = f32[320,768]{1,0:T(8,128)S(1)} collective-permute-done((f32[320,768]{1,0:T(8,128)}, f32[320,768]{1,0:T(8,128)S(1)}, u32[]{:S(2)}, u32[]{:S(2)}) %collective-permute-start.105) | collective-permute-done | bytes 983072 | tf_op jit(solution)/shard_map/ppermute | solution.py:321
  990.6 21.2 %collective-permute-done.130 = f32[128,2048]{1,0:T(8,128)S(1)} collective-permute-done((f32[128,2048]{1,0:T(8,128)S(1)}, f32[128,2048]{1,0:T(8,128)S(1)}, u32[]{:S(2)}, u32[]{:S(2)}) %collective-permute-start.130) | collective-permute-done | bytes 1048608 | tf_op jit(solution)/shard_map/ppermute | solution.py:321
  1013.8 35.4 %fusion.10 = (f32[2048]{0:T(1024)S(1)}, f32[4,256]{1,0:T(4,128)S(1)}, f32[4,256]{1,0:T(4,128)S(1)}, f32[2048]{0:T(1024)S(1)}, f32[4,256,2048]{2,1,0:T(8,128)S(1)}) fusion(bf16[4,256,2048]{2,1,0:T(8,128)(2,1)S(1)} %copy-done.2, f32[4,256]{1,0:T(4,128)} %add_rsqrt_fusion, f32[4,256]{1,0:T(4,128)S(1)} %broadcast_multiply_fusion.2, f32[2048]{0:T(1024)S(1)} %copy-done.81, ...), kind=kOutput, calls=%fused_computation.17 | convolution fusion | flops 25790769152 | bytes 50372608 | tf_op jit(solution)/shard_map/bsk,hk->bsh/dot_general | solution.py:395
  1077.8 13.9 %fusion.13 = bf16[4,256,2048]{2,1,0:T(8,128)(2,1)} fusion(bf16[4,256,2048]{2,1,0:T(8,128)(2,1)S(1)} %copy-done.2, f32[2048]{0:T(1024)S(1)} %copy-done.110, bf16[4,256,2048]{2,1,0:T(8,128)(2,1)} %bitcast.153, bf16[2048,2048]{1,0:T(8,128)(2,1)} %param.17), kind=kOutput, calls=%fused_computation.20 | convolution fusion | flops 8598323200 | bytes 20979712 | tf_op jit(solution)/shard_map/bsh,hk->bsk/dot_general | solution.py:394
  1111.3 13.5 %stack_rows.1 = f32[8,256,2048]{2,1,0:T(8,128)} custom-call(s32[1]{0:T(128)} %bitcast.me_ref, f32[256,2048]{1,0:T(8,128)} %get-tuple-element.74.refs_0_, f32[256,2048]{1,0:T(8,128)} %collective-permute-done.125.refs_1_, f32[256,2048]{1,0:T(8,128)} %collective-permute-done.126.refs_2_, f32[256,2048]{1,0:T(8,128)} %collective-permute-done.127.refs_3_, ...), custom_call_target="tpu_custom_call" | custom-call | flops 16777216 | bytes 33554432 | tf_op jit(solution)/shard_map/stack_rows/pallas_call | solution.py:296
  (606 shorter events, 387.4 us)
Async XLA Ops:
  7.5 69.3 %collective-permute-start.7 = (bf16[256,2048]{1,0:T(8,128)(2,1)S(1)}, bf16[256,2048]{1,0:T(8,128)(2,1)}, u32[]{:S(2)}, u32[]{:S(2)}) collective-permute-start(bf16[256,2048]{1,0:T(8,128)(2,1)S(1)} %get-tuple-element.115.refs_0_), channel_id=1, source_target_pairs={{0,2},{1,3},{2,0},{3,1},{4,6},{5,7},{6,4},{7,5}} | collective-permute-start | bytes 3145736 | tf_op jit(solution)/shard_map/ppermute | solution.py:321
  10.8 66.0 %collective-permute-start.8 = (bf16[256,2048]{1,0:T(8,128)(2,1)S(1)}, bf16[256,2048]{1,0:T(8,128)(2,1)S(1)}, u32[]{:S(2)}, u32[]{:S(2)}) collective-permute-start(bf16[256,2048]{1,0:T(8,128)(2,1)S(1)} %get-tuple-element.115.refs_0_), channel_id=1, source_target_pairs={{0,4},{1,5},{2,6},{3,7},{4,0},{5,1},{6,2},{7,3}} | collective-permute-start | bytes 3145736 | tf_op jit(solution)/shard_map/ppermute | solution.py:321
  12.3 65.9 %collective-permute-start.11 = (bf16[256,2048]{1,0:T(8,128)(2,1)S(1)}, bf16[256,2048]{1,0:T(8,128)(2,1)S(1)}, u32[]{:S(2)}, u32[]{:S(2)}) collective-permute-start(bf16[256,2048]{1,0:T(8,128)(2,1)S(1)} %get-tuple-element.115.refs_0_), channel_id=1, source_target_pairs={{0,1},{1,0},{2,3},{3,2},{4,5},{5,4},{6,7},{7,6}} | collective-permute-start | bytes 3145736 | tf_op jit(solution)/shard_map/ppermute | solution.py:321
  13.0 65.8 %collective-permute-start.16 = (bf16[256,2048]{1,0:T(8,128)(2,1)S(1)}, bf16[256,2048]{1,0:T(8,128)(2,1)S(1)}, u32[]{:S(2)}, u32[]{:S(2)}) collective-permute-start(bf16[256,2048]{1,0:T(8,128)(2,1)S(1)} %get-tuple-element.129.refs_10_), channel_id=1, source_target_pairs={{0,2},{1,3},{2,0},{3,1},{4,6},{5,7},{6,4},{7,5}} | collective-permute-start | bytes 3145736 | tf_op jit(solution)/shard_map/ppermute | solution.py:321
  410.9 74.4 %all-to-all-start = ((bf16[8,256,1024]{2,1,0:T(8,128)(2,1)}), bf16[8,256,1024]{2,1,0:T(8,128)(2,1)}, u32[]{:S(2)}, u32[]{:S(2)}) async-start(bf16[8,256,1024]{2,1,0:T(8,128)(2,1)} %bitcast.148), calls=%async_computation | async-start | bytes 8388608 | tf_op jit(solution)/shard_map/all_to_all | solution.py:380
  485.3 186.3 %all-to-all-start.1 = ((bf16[8,256,1024]{2,1,0:T(8,128)(2,1)}), bf16[8,256,1024]{2,1,0:T(8,128)(2,1)}, u32[]{:S(2)}, u32[]{:S(2)}) async-start(bf16[8,256,1024]{2,1,0:T(8,128)(2,1)} %bitcast.149), calls=%async_computation.1 | async-start | bytes 8388608 | tf_op jit(solution)/shard_map/all_to_all | solution.py:380
  606.8 156.1 %collective-permute-start.102 = (f32[640,768]{1,0:T(8,128)}, f32[640,768]{1,0:T(8,128)}, u32[]{:S(2)}, u32[]{:S(2)}) collective-permute-start(f32[640,768]{1,0:T(8,128)} %slice.205.p0), channel_id=1, source_target_pairs={{0,4},{1,5},{2,6},{3,7},{4,0},{5,1},{6,2},{7,3}} | collective-permute-start | bytes 5898248 | tf_op jit(solution)/shard_map/ppermute | solution.py:321
  614.2 80.7 %collective-permute-start.94 = (f32[384,768]{1,0:T(8,128)S(1)}, f32[384,768]{1,0:T(8,128)}, u32[]{:S(2)}, u32[]{:S(2)}) collective-permute-start(f32[384,768]{1,0:T(8,128)S(1)} %slice.202.p0), channel_id=1, source_target_pairs={{0,4},{1,5},{2,6},{3,7},{4,0},{5,1},{6,2},{7,3}} | collective-permute-start | bytes 3538952 | tf_op jit(solution)/shard_map/ppermute | solution.py:321
  615.8 81.2 %collective-permute-start.96 = (f32[384,768]{1,0:T(8,128)S(1)}, f32[384,768]{1,0:T(8,128)S(1)}, u32[]{:S(2)}, u32[]{:S(2)}) collective-permute-start(f32[384,768]{1,0:T(8,128)S(1)} %slice.202.p0), channel_id=1, source_target_pairs={{0,2},{1,3},{2,0},{3,1},{4,6},{5,7},{6,4},{7,5}} | collective-permute-start | bytes 3538952 | tf_op jit(solution)/shard_map/ppermute | solution.py:321
  671.7 264.4 %all-to-all-start.2 = ((bf16[8,256,1024]{2,1,0:T(8,128)(2,1)}), bf16[8,256,1024]{2,1,0:T(8,128)(2,1)}, u32[]{:S(2)}, u32[]{:S(2)}) async-start(bf16[8,256,1024]{2,1,0:T(8,128)(2,1)} %bitcast.150), calls=%async_computation.2 | async-start | bytes 8388608 | tf_op jit(solution)/shard_map/all_to_all | solution.py:380
  748.2 143.3 %collective-permute-start.117 = (f32[768,768]{1,0:T(8,128)S(1)}, f32[768,768]{1,0:T(8,128)S(1)}, u32[]{:S(2)}, u32[]{:S(2)}) collective-permute-start(f32[768,768]{1,0:T(8,128)S(1)} %slice.217.p0), channel_id=1, source_target_pairs={{0,4},{1,5},{2,6},{3,7},{4,0},{5,1},{6,2},{7,3}} | collective-permute-start | bytes 7077896 | tf_op jit(solution)/shard_map/ppermute | solution.py:321
  750.2 144.3 %collective-permute-start.119 = (f32[768,768]{1,0:T(8,128)S(1)}, f32[768,768]{1,0:T(8,128)S(1)}, u32[]{:S(2)}, u32[]{:S(2)}) collective-permute-start(f32[768,768]{1,0:T(8,128)S(1)} %slice.217.p0), channel_id=1, source_target_pairs={{0,2},{1,3},{2,0},{3,1},{4,6},{5,7},{6,4},{7,5}} | collective-permute-start | bytes 7077896 | tf_op jit(solution)/shard_map/ppermute | solution.py:321
  760.9 85.7 %collective-permute-start.104 = (f32[640,768]{1,0:T(8,128)}, f32[640,768]{1,0:T(8,128)}, u32[]{:S(2)}, u32[]{:S(2)}) collective-permute-start(f32[640,768]{1,0:T(8,128)} %slice.205.p0), channel_id=1, source_target_pairs={{0,2},{1,3},{2,0},{3,1},{4,6},{5,7},{6,4},{7,5}} | collective-permute-start | bytes 5898248 | tf_op jit(solution)/shard_map/ppermute | solution.py:321
  762.8 128.7 %collective-permute-start.126 = (f32[256,2048]{1,0:T(8,128)}, f32[256,2048]{1,0:T(8,128)}, u32[]{:S(2)}, u32[]{:S(2)}) collective-permute-start(f32[256,2048]{1,0:T(8,128)} %get-tuple-element.74.refs_0_), channel_id=1, source_target_pairs={{0,2},{1,3},{2,0},{3,1},{4,6},{5,7},{6,4},{7,5}} | collective-permute-start | bytes 6291464 | tf_op jit(solution)/shard_map/ppermute | solution.py:321
  762.9 128.7 %collective-permute-start.128 = (f32[256,2048]{1,0:T(8,128)}, f32[256,2048]{1,0:T(8,128)}, u32[]{:S(2)}, u32[]{:S(2)}) collective-permute-start(f32[256,2048]{1,0:T(8,128)} %get-tuple-element.74.refs_0_), channel_id=1, source_target_pairs={{0,4},{1,5},{2,6},{3,7},{4,0},{5,1},{6,2},{7,3}} | collective-permute-start | bytes 6291464 | tf_op jit(solution)/shard_map/ppermute | solution.py:321
  940.2 72.1 %collective-permute-start.120 = (f32[384,768]{1,0:T(8,128)S(1)}, f32[384,768]{1,0:T(8,128)S(1)}, u32[]{:S(2)}, u32[]{:S(2)}) collective-permute-start(f32[384,768]{1,0:T(8,128)S(1)} %copy-done.22), channel_id=1, source_target_pairs={{0,4},{1,5},{2,6},{3,7},{4,0},{5,1},{6,2},{7,3}} | collective-permute-start | bytes 3538952 | tf_op jit(solution)/shard_map/ppermute | solution.py:321
  990.1 84.0 %collective-permute-start.103 = (f32[640,768]{1,0:T(8,128)}, f32[640,768]{1,0:T(8,128)}, u32[]{:S(2)}, u32[]{:S(2)}) collective-permute-start(f32[640,768]{1,0:T(8,128)} %collective-permute-done.102.p0), channel_id=1, source_target_pairs={{0,1},{1,0},{2,3},{3,2},{4,5},{5,4},{6,7},{7,6}} | collective-permute-start | bytes 5898248 | tf_op jit(solution)/shard_map/ppermute | solution.py:321
  990.1 84.5 %collective-permute-start.116 = (f32[640,768]{1,0:T(8,128)}, f32[640,768]{1,0:T(8,128)}, u32[]{:S(2)}, u32[]{:S(2)}) collective-permute-start(f32[640,768]{1,0:T(8,128)} %collective-permute-done.104.p2), channel_id=1, source_target_pairs={{0,1},{1,0},{2,3},{3,2},{4,5},{5,4},{6,7},{7,6}} | collective-permute-start | bytes 5898248 | tf_op jit(solution)/shard_map/ppermute | solution.py:321
  1011.8 66.0 %collective-permute-start.129 = (f32[256,2048]{1,0:T(8,128)}, f32[256,2048]{1,0:T(8,128)}, u32[]{:S(2)}, u32[]{:S(2)}) collective-permute-start(f32[256,2048]{1,0:T(8,128)} %collective-permute-done.128.refs_4_), channel_id=1, source_target_pairs={{0,1},{1,0},{2,3},{3,2},{4,5},{5,4},{6,7},{7,6}} | collective-permute-start | bytes 6291464 | tf_op jit(solution)/shard_map/ppermute | solution.py:321
  1091.8 76.2 %collective-permute-start.92 = (f32[256,768]{1,0:T(8,128)}, f32[256,768]{1,0:T(8,128)}, u32[]{:S(2)}, u32[]{:S(2)}) collective-permute-start(f32[256,768]{1,0:T(8,128)} %slice.199.p0), channel_id=1, source_target_pairs={{0,1},{1,0},{2,3},{3,2},{4,5},{5,4},{6,7},{7,6}} | collective-permute-start | bytes 2359304 | tf_op jit(solution)/shard_map/ppermute | solution.py:321
  1092.2 80.2 %collective-permute-start.87 = (f32[256,768]{1,0:T(8,128)}, f32[256,768]{1,0:T(8,128)}, u32[]{:S(2)}, u32[]{:S(2)}) collective-permute-start(f32[256,768]{1,0:T(8,128)} %collective-permute-done.86.p0), channel_id=1, source_target_pairs={{0,1},{1,0},{2,3},{3,2},{4,5},{5,4},{6,7},{7,6}} | collective-permute-start | bytes 2359304 | tf_op jit(solution)/shard_map/ppermute | solution.py:321
  1092.3 75.7 %collective-permute-start.93 = (f32[256,768]{1,0:T(8,128)}, f32[256,768]{1,0:T(8,128)}, u32[]{:S(2)}, u32[]{:S(2)}) collective-permute-start(f32[256,768]{1,0:T(8,128)} %collective-permute-done.88.p2), channel_id=1, source_target_pairs={{0,1},{1,0},{2,3},{3,2},{4,5},{5,4},{6,7},{7,6}} | collective-permute-start | bytes 2359304 | tf_op jit(solution)/shard_map/ppermute | solution.py:321
  1092.7 79.7 %collective-permute-start.91 = (f32[256,768]{1,0:T(8,128)}, f32[256,768]{1,0:T(8,128)}, u32[]{:S(2)}, u32[]{:S(2)}) collective-permute-start(f32[256,768]{1,0:T(8,128)} %constant_dynamic-update-slice_fusion.8.p2), channel_id=1, source_target_pairs={{0,1},{1,0},{2,3},{3,2},{4,5},{5,4},{6,7},{7,6}} | collective-permute-start | bytes 2359304 | tf_op jit(solution)/shard_map/ppermute | solution.py:321
  1092.8 68.7 %collective-permute-start.99 = (f32[384,768]{1,0:T(8,128)}, f32[384,768]{1,0:T(8,128)}, u32[]{:S(2)}, u32[]{:S(2)}) collective-permute-start(f32[384,768]{1,0:T(8,128)} %constant_dynamic-update-slice_fusion.10.p2), channel_id=1, source_target_pairs={{0,1},{1,0},{2,3},{3,2},{4,5},{5,4},{6,7},{7,6}} | collective-permute-start | bytes 3538952 | tf_op jit(solution)/shard_map/ppermute | solution.py:321
  (223 other events, 8254.8 us)
